TPU v7x, 32 devices: a whole 2x2x4 slice. The times are simulated.
32 devices in a mesh: gx: 2 (over x), gy: 4 (over y, core), gz: 4 (over z).
Axes of the slice: x: 2, y: 2, z: 4, core: 2. Of those that a mesh axis runs over, the one named last changes fastest.
Arguments:
- panels: bfloat16 [3072, 8192], P(('gx', 'gy'), 'gz'), may hold values from -0.75 to 0.75
- sizes: int32 [8], replicated, may hold values from 1 to 1024
- front: float32 [3072, 3072], P(('gx', 'gz'), 'gy'), may hold values from -6 to 6
Outputs:
- updated: float32 [3072, 3072], P(('gx', 'gz'), 'gy')
All inputs are finite; a program needn't handle non-finite values.
Results may differ from a plain program's by a relative error of at most 0.0003.
Values may be sent and summed in bfloat16 or wider, within the bound.
No kernel may reach another device: no remote copies, remote signals or barrier semaphores. Data moves between devices by JAX's collectives and lax.ppermute only.
A program may use at most 128 MiB of HBM per device.

v0:
```python
import jax
import jax.numpy as jnp
from jax import lax
from jax.sharding import PartitionSpec as P

WIDTH = 1024


def shards(panels, sizes, front):
    piece_rows = panels.shape[0]
    panel_count = panels.shape[1] // WIDTH
    first = lax.axis_index("gz") * panel_count
    limits = lax.dynamic_slice_in_dim(sizes, first, panel_count, 0)
    column = jnp.arange(WIDTH, dtype=jnp.int32)
    live = (column[None, :] < limits[:, None]).reshape(panel_count * WIDTH).astype(jnp.bfloat16)
    gathered = lax.all_gather(panels, ("gx", "gy"), axis=0, tiled=True)
    count_x = lax.axis_size("gx")
    count_y = lax.axis_size("gy")
    block_rows = piece_rows * count_y
    row_part = lax.dynamic_slice_in_dim(gathered, lax.axis_index("gx") * block_rows, block_rows, 0)
    grouped = gathered.reshape(count_x, count_y, piece_rows, panels.shape[1])
    column_part = lax.dynamic_index_in_dim(grouped, lax.axis_index("gy"), 1, keepdims=False)
    column_part = column_part.reshape(count_x * piece_rows, panels.shape[1])
    masked = row_part * live[None, :]
    summed = lax.psum_scatter(
        -lax.dot_general(
            masked, column_part, (((1,), (1,)), ((), ())), preferred_element_type=jnp.float32
        ),
        "gz",
        scatter_dimension=0,
        tiled=True,
    )
    return front + summed


def solution(mesh):
    in_specs = (P(("gx", "gy"), "gz"), P(), P(("gx", "gz"), "gy"))
    out_specs = P(("gx", "gz"), "gy")
    return jax.shard_map(shards, mesh=mesh, in_specs=in_specs, out_specs=out_specs, check_vma=False)
```

profile of v0, /device:TPU:0, one launch (start us, length us, event | category | flops | bytes accessed | tf_op | source)
XLA Modules:
  0.0 189.4 jit_solution(4549865827365478401)
XLA Ops:
  6.5 0.0 all-gather.2.cloned.1.call-start
  6.5 0.7 all-gather.2.cloned.1.call-update
  7.3 0.0 reduce-scatter.2.cloned.1.call-start
  7.3 0.7 dynamic_slice.11
  8.0 0.1 fusion.7
  8.1 75.8 %all-gather.2.cloned.1.call-done = bf16[3072,2048]{1,0:T(8,128)(2,1)} async-done(((bf16[384,2048]{1,0:T(8,128)(2,1)}), bf16[3072,2048]{1,0:T(8,128)(2,1)}) %all-gather.2.cloned.1.call-update) | async-done | bytes 12582928 | tf_op jit(solution)/shard_map/all_gather | solution.py:16
  84.0 2.1 %constant_dynamic-slice_fusion = bf16[2,1,384,2048]{3,2,1,0:T(8,128)(2,1)S(1)} fusion(bf16[2,4,384,2048]{3,2,1,0:T(8,128)(2,1)} %bitcast.9, s32[]{:T(128)S(6)} %select_n.12), kind=kLoop, calls=%fused_computation.8 | loop fusion | bytes 6291460 | tf_op jit(solution)/shard_map/jit(dynamic_index_in_dim)/dynamic_slice | solution.py:22
  86.1 8.6 %fusion.3 = f32[1536,768]{1,0:T(8,128)} fusion(bf16[768,2048]{1,0:T(8,128)(2,1)S(1)} %bitcast.8, bf16[3072,2048]{1,0:T(8,128)(2,1)} %all-gather.2.cloned.1.call-done, s32[]{:T(128)S(6)} %select_n.10, bf16[2048]{0:T(1024)(128)(2,1)S(1)} %bitcast.10), kind=kOutput, calls=%fused_computation.3 | convolution fusion | flops 4845600768 | bytes 14159876 | tf_op jit(solution)/shard_map/dot_general | solution.py:26
  94.7 0.0 copy-start
  94.7 0.0 reduce-scatter.2.cloned.1.call-update
  94.7 85.4 %reduce-scatter.2.cloned.1.call-done = f32[384,768]{1,0:T(8,128)} async-done(((f32[1536,768]{1,0:T(8,128)}), f32[384,768]{1,0:T(8,128)}) %reduce-scatter.2.cloned.1.call-update) | async-done | bytes 1179664 | tf_op jit(solution)/shard_map/reduce_scatter | solution.py:25
  180.2 0.0 copy-done
  180.2 2.4 %add.18 = f32[384,768]{1,0:T(8,128)} add(f32[384,768]{1,0:T(8,128)S(1)} %copy-done, f32[384,768]{1,0:T(8,128)} %reduce-scatter.2.cloned.1.call-done) | non-fusion elementwise | flops 294912 | bytes 3538944 | tf_op jit(solution)/shard_map/add | solution.py:33
  (1 shorter events, 0.0 us)
Async XLA Ops:
  6.5 77.4 %all-gather.2.cloned.1.call-start = ((), (), s32[]{:S(2)}) async-start(), calls=%async_computation.1 | async-start | bytes 14155776 | tf_op jit(solution)/shard_map/all_gather | solution.py:16
  7.3 172.9 %reduce-scatter.2.cloned.1.call-start = ((), (), s32[]{:S(2)}) async-start(), calls=%async_computation.2 | async-start | bytes 5898240 | tf_op jit(solution)/shard_map/reduce_scatter | solution.py:25
  94.7 85.5 %copy-start = (f32[384,768]{1,0:T(8,128)S(1)}, f32[384,768]{1,0:T(8,128)}, u32[]{:S(2)}) copy-start(f32[384,768]{1,0:T(8,128)} %param.5) | copy-start | bytes 3538948
Sparse Core Ops, SparseCore 0:
  9.2 74.7 all-gather.1
  94.9 85.2 reduce-scatter.1
where the time goes:
time: 190 us; the launch traced here: 189 us
  waiting for transfers between devices  162 us (85%)
  between operations  13.4 us (7%)
  matrix products  8.63 us (5%)
  local copies, waits for them, and re-layouts  2.85 us (2%)
  other arithmetic  2.5 us (1%)
    reduce_scatter x1, waiting for transfers between devices, shards(): lax.psum_scatter(-lax.dot_general(masked, column_part, (((1,), (1,)), (()...  85.4 us
    all_gather x1, waiting for transfers between devices, shards(): gathered = lax.all_gather(panels, ('gx', 'gy'), axis=0, tiled=True)  75.8 us
    dot_general x1, matrix products, shards(): lax.dot_general(masked, column_part, (((1,), (1,)), ((), ())), preferred_...  8.63 us
  transfers between devices with their start and end apart: 2, of which 2 were waited for; matrix products, arithmetic and copies ran while one was open for 0% of the time, Pallas kernels for 0%

commit v1 on v0

--- a/solution.py
+++ b/solution.py
@@ -1,12 +1,21 @@
+import functools
+
 import jax
 import jax.numpy as jnp
 from jax import lax
+from jax.experimental import pallas as pl
+from jax.experimental.pallas import tpu as pltpu
 from jax.sharding import PartitionSpec as P
 
+
 WIDTH = 1024
-
-
-def shards(panels, sizes, front):
+GROUP = 64
+CODES = 16
+STEPS = 256.0
+TOP = 32767.0
+
+
+def plain(panels, sizes, front):
     piece_rows = panels.shape[0]
     panel_count = panels.shape[1] // WIDTH
     first = lax.axis_index("gz") * panel_count
@@ -33,7 +42,342 @@
     return front + summed
 
 
+def place(rnd, n):
+    g = lax.axis_index("gy")
+    z = lax.axis_index("gz")
+    own_half = g // (n // 2)
+    half = own_half if rnd == 0 else 1 - own_half
+    w = jnp.where(half == 1, z, n - 1 - z)
+    far = jnp.where(half == 1, n - 1, 0)
+    return g, w, far
+
+
+def product(rows, cols_ref, live_ref):
+    return lax.dot_general(
+        rows * live_ref[...], cols_ref[...], (((1,), (1,)), ((), ())), preferred_element_type=jnp.float32
+    )
+
+
+def decode(packet_ref, group, codes):
+    scale = jnp.exp2(codes[group : group + 1, :] * (1.0 / STEPS)) * (1.0 / TOP)
+    values = packet_ref[group * GROUP : (group + 1) * GROUP, :].astype(jnp.int32).astype(jnp.float32)
+    return values * scale
+
+
+def read_codes(packet_ref):
+    height = packet_ref.shape[0] - CODES
+    return packet_ref[height:, :].astype(jnp.int32).astype(jnp.float32)
+
+
+def encode(out_ref, read):
+    height, width = out_ref.shape[0] - CODES, out_ref.shape[1]
+    line = lax.broadcasted_iota(jnp.int32, (CODES, width), 0)
+    codes = jnp.zeros((CODES, width), jnp.float32)
+    for group in range(height // GROUP):
+        part = read(group)
+        most = jnp.max(jnp.abs(part), axis=0, keepdims=True)
+        code = jnp.ceil(jnp.log2(jnp.maximum(most, 1e-30)) * STEPS) + 1.0
+        scaled = jnp.round(part * (jnp.exp2(code * (-1.0 / STEPS)) * TOP))
+        scaled = jnp.clip(scaled, -TOP, TOP)
+        out_ref[group * GROUP : (group + 1) * GROUP, :] = scaled.astype(jnp.int32).astype(jnp.int16)
+        codes = jnp.where(line == group, code, codes)
+    out_ref[height:, :] = codes.astype(jnp.int32).astype(jnp.int16)
+
+
+def rows_of(group):
+    return slice(group * GROUP, (group + 1) * GROUP)
+
+
+def rows_of(group):
+    return slice(group * GROUP, (group + 1) * GROUP)
+
+
+def headed(to, n):
+    g = lax.axis_index("gy")
+    return jnp.where(g // (n // 2) == to // (n // 2), 0, 1)
+
+
+def at_ends(n):
+    g = lax.axis_index("gy")
+    return (g == 0) | (g == n - 1)
+
+
+def own_kernel(n, live, panels, beside, cols, sums, packet):
+    g, w, far = place(0, n)
+    sums[0] = product(panels[...], cols, live)
+    sums[1] = product(beside[...], cols, live)
+    at = jnp.where((g == far) == (w == 0), 0, 1)
+    encode(packet, lambda group: sums[at, rows_of(group), :])
+
+
+def own_step_kernel(step, n, sums, held, packet):
+    g, w, far = place(0, n)
+
+    @pl.when((w <= step) & (w >= step - 1))
+    def _():
+        codes = read_codes(held)
+        at = jnp.where((g == far) == (w == step), 0, 1)
+        encode(packet, lambda group: sums[at, rows_of(group), :] + decode(held, group, codes))
+
+
+def other_kernel(kind, n, live, first, second, cols, sums, packet):
+    pick = at_ends(n) == (kind == "near")
+    sums[...] = product(jnp.where(pick, first[...], second[...]), cols, live)
+    encode(packet, lambda group: sums[rows_of(group), :])
+
+
+def other_step_kernel(step, n, sums, held, packet):
+    _, w, _ = place(1, n)
+
+    @pl.when(w == step)
+    def _():
+        codes = read_codes(held)
+        encode(packet, lambda group: sums[rows_of(group), :] + decode(held, group, codes))
+
+
+def both_kernel(kind, n, live, panels, beside, first, second, cols, sums, *packets):
+    z = lax.axis_index("gz")
+    ends = at_ends(n)
+    near = kind == "near"
+    top = n - 2 if near else n - 1
+    sums[0] = product(jnp.where(ends != near, panels[...], beside[...]), cols, live)
+    sums[1] = product(jnp.where(ends == near, first[...], second[...]), cols, live)
+    for index, packet in enumerate(packets):
+
+        @pl.when((z == 0) | (z == n - 1))
+        def _(index=index, packet=packet):
+            up = (z == 0) == (index == 0)
+            at = jnp.where(up, headed(top, n), headed(n - 1 - top, n))
+            encode(packet, lambda group: sums[at, rows_of(group), :])
+
+
+def both_step_kernel(kind, step, n, sums, held, packet):
+    z = lax.axis_index("gz")
+    top = n - 2 if kind == "near" else n - 1
+
+    @pl.when((z == step) | (z == n - 1 - step))
+    def _():
+        codes = read_codes(held)
+        at = jnp.where(z == step, headed(top, n), headed(n - 1 - top, n))
+        encode(packet, lambda group: sums[at, rows_of(group), :] + decode(held, group, codes))
+
+
+VMEM = pl.BlockSpec(memory_space=pltpu.VMEM)
+
+
+def call(kernel, outs, operands, flops):
+    size = sum(v.size * v.dtype.itemsize for v in (*operands, *outs))
+    return pl.pallas_call(
+        kernel,
+        out_shape=outs if len(outs) > 1 else outs[0],
+        in_specs=[VMEM] * len(operands),
+        out_specs=[VMEM] * len(outs) if len(outs) > 1 else VMEM,
+        compiler_params=pltpu.CompilerParams(vmem_limit_bytes=min(size + (4 << 20), 60 << 20)),
+        cost_estimate=pl.CostEstimate(flops=flops, bytes_accessed=size, transcendentals=0),
+    )(*operands)
+
+
+def base_kernel(n, count_x, front, *rest):
+    sums, out_ref = rest[:-1], rest[-1]
+    x = lax.axis_index("gx")
+    z = lax.axis_index("gz")
+    rows = front.shape[0]
+    g, w, far = place(0, n)
+
+    def columns(d):
+        return pl.ds(pl.multiple_of(lax.rem(x + d, count_x) * rows, 128), rows)
+
+    @pl.when(w >= n // 2)
+    def _():
+        at = jnp.where((g == far) == (w == n - 1), 0, 1)
+        out_ref[:, columns(0)] = front[:, columns(0)] - sums[0][at]
+
+    for at_w, index in ((0, 1), (1, 2)):
+
+        @pl.when(w == at_w)
+        def _(index=index):
+            out_ref[:, columns(0)] = front[:, columns(0)] - sums[index][...]
+
+    edge = (z == 0) | (z == n - 1)
+    for d in range(1, count_x):
+        for side, index in ((edge, 1 + 2 * d), (jnp.logical_not(edge), 2 + 2 * d)):
+
+            @pl.when(side)
+            def _(d=d, index=index):
+                mine = jnp.where(w >= n // 2, 0, 1)
+                out_ref[:, columns(d)] = front[:, columns(d)] - sums[index][mine]
+
+
+def final_kernel(n, count_x, base, *rest):
+    packets, out_ref = rest[:-1], rest[-1]
+    x = lax.axis_index("gx")
+    z = lax.axis_index("gz")
+    rows = base.shape[0]
+    _, w, _ = place(0, n)
+
+    def finish(d, picks):
+        columns = pl.ds(pl.multiple_of(lax.rem(x + d, count_x) * rows, 128), rows)
+        refs = [packets[k] for k in picks]
+        codes = [read_codes(ref) for ref in refs]
+        for group in range(rows // GROUP):
+            value = base[rows_of(group), columns]
+            for ref, code in zip(refs, codes):
+                value = value - decode(ref, group, code)
+            out_ref[rows_of(group), columns] = value
+
+    for at, picks in ((n - 1, (1,)), (n - 2, (0, 1)), (0, (2,)), (1, (3, 4))):
+
+        @pl.when(w == at)
+        def _(picks=picks):
+            finish(0, picks)
+
+    edge = (z == 0) | (z == n - 1)
+    for d in range(1, count_x):
+        for side, picks in ((edge, (2 + 3 * d,)), (jnp.logical_not(edge), (3 + 3 * d, 4 + 3 * d))):
+
+            @pl.when(side)
+            def _(d=d, picks=picks):
+                finish(d, picks)
+
+
+def plan(count_x):
+    crossed = range(1, count_x)
+
+    def go(label, step):
+        return [f"{label}_k{step}", f">{label}_{step}"]
+
+    names = [">beside", ">far0"] + [f">cross{d}" for d in crossed] + [">near0"]
+    names += go("own", 0) + go("own", 1) + [">far1"] + go("far", 0) + go("own", 2)
+    for d in crossed:
+        names += go(f"xf{d}", 0)
+    names += [">near1"] + go("far", 1)
+    for d in crossed:
+        names += go(f"xn{d}", 0)
+    names += go("near", 0)
+    for d in crossed:
+        names += [f">xn{d}_x"]
+    for d in crossed:
+        names += go(f"xf{d}", 1)
+    names += go("far", 2)
+    for d in crossed:
+        names += go(f"xn{d}", 1)
+    for d in crossed:
+        names += go(f"xf{d}", 2)
+    return names + go("near", 1) + ["base", "final"]
+
+
+def shards(n, count_x, panels, sizes, front):
+    rows, width = panels.shape
+    square = 2 * rows * rows * width
+    sums1 = jax.ShapeDtypeStruct((rows, rows), jnp.float32)
+    sums2 = jax.ShapeDtypeStruct((2, rows, rows), jnp.float32)
+    packet = jax.ShapeDtypeStruct((rows + CODES, rows), jnp.int16)
+    block = jax.ShapeDtypeStruct(front.shape, jnp.float32)
+
+    def move(value, axes, pairs):
+        return lax.ppermute(value, axes, pairs)
+
+    def way(rnd, hops):
+        pairs = []
+        for g in range(n):
+            half = g // (n // 2) if rnd == 0 else 1 - g // (n // 2)
+            for a, b in hops:
+                source, target = (a, b) if half == 1 else (n - 1 - a, n - 1 - b)
+                pairs.append((g * n + source, g * n + target))
+        return pairs
+
+    def both(hop):
+        return way(0, [hop]) + way(1, [hop])
+
+    count = width // WIDTH
+    here = jnp.arange(sizes.size, dtype=jnp.int32)[:, None] == lax.axis_index("gz") * count + jnp.arange(count)[None, :]
+    limits = jnp.sum(jnp.where(here, sizes[:, None], 0), axis=0)
+    live = (jnp.arange(WIDTH)[None, :] < limits[:, None]).reshape(1, width).astype(jnp.bfloat16)
+
+    hops = {
+        "own_0": way(0, [(0, 1), (n - 1, n - 2)]),
+        "own_1": way(0, [(0, 1), (1, 2)]),
+        "own_2": way(0, [(1, 2), (2, 3)]),
+        "far_0": way(1, [(0, 1)]),
+        "far_1": way(1, [(1, 2)]),
+        "far_2": way(1, [(2, 3)]),
+        "near_0": way(1, [(0, 1), (n - 1, n - 2)]),
+        "near_1": way(1, [(1, 2)]),
+        "xf_0": both((0, 1)),
+        "xf_1": both((1, 2)),
+        "xf_2": both((2, 3)),
+        "xn_0": both((0, 1)),
+        "xn_1": both((1, 2)),
+        "xn_x": both((n - 1, n - 2)),
+    }
+    y_moves = {
+        "beside": (None, [(g, g ^ 1) for g in range(n)]),
+        "far0": (None, [(0, 2), (3, 1)]),
+        "near0": ("beside", [(0, 3), (3, 0)]),
+        "far1": ("far0", [(2, 3), (1, 0)]),
+        "near1": ("near0", [(3, 2), (0, 1)]),
+    }
+    held = {}
+    sums = {}
+    sent = {}
+    got = {}
+    for name in plan(count_x):
+        label = name.lstrip(">")
+        part, _, step = label.partition("_")
+        step = step.lstrip("k")
+        kind, d = part.rstrip("0123456789"), int("0" + part.lstrip("abcdefghijklmnopqrstuvwxyz"))
+        if label in y_moves:
+            source, pairs = y_moves[label]
+            held[label] = move(panels if source is None else held[source], "gy", pairs)
+        elif kind == "cross":
+            held[label] = move(panels, "gx", [((i + d) % count_x, i) for i in range(count_x)])
+        elif name[0] == ">":
+            got[label] = move(sent[label], ("gy", "gz"), hops[f"{kind}_{step}"])
+        elif label == "base":
+            each = [sums[k] for k in ("own", "far", "near")]
+            each += [sums[f"{k}{d}"] for d in range(1, count_x) for k in ("xf", "xn")]
+            base = call(functools.partial(base_kernel, n, count_x), [block], [front, *each], 1)
+        elif label == "final":
+            each = [got[k] for k in ("own_0", "own_2", "far_2", "near_0", "near_1")]
+            for d in range(1, count_x):
+                each += [got[f"xf{d}_2"], got[f"xn{d}_1"], got[f"xn{d}_x"]]
+            return call(functools.partial(final_kernel, n, count_x), [block], [base, *each], 1)
+        elif step == "0":
+            cols = held[f"cross{d}"] if d else panels
+            local = (panels, held["beside"])
+            other = () if kind == "own" else (held["far0"], held["far1"])
+            if kind in ("near", "xn"):
+                other = (held["near0"], held["near1"])
+            if kind == "own":
+                kernel, pieces, outs = functools.partial(own_kernel, n), local, [sums2, packet]
+            elif kind in ("far", "near"):
+                kernel, pieces, outs = functools.partial(other_kernel, kind, n), other, [sums1, packet]
+            else:
+                kernel = functools.partial(both_kernel, "far" if kind == "xf" else "near", n)
+                pieces, outs = (*local, *other), [sums2, packet] + [packet] * (kind == "xn")
+            done = call(kernel, outs, [live, *pieces, cols], len(pieces) * square // 2)
+            sums[part], sent[f"{part}_0"] = done[:2]
+            sent[f"{part}_x"] = done[-1]
+        else:
+            kernel = {
+                "own": functools.partial(own_step_kernel, int(step), n),
+                "far": functools.partial(other_step_kernel, int(step), n),
+                "near": functools.partial(other_step_kernel, int(step), n),
+                "xf": functools.partial(both_step_kernel, "far", int(step), n),
+                "xn": functools.partial(both_step_kernel, "near", int(step), n),
+            }[kind]
+            held_now = got[f"{part}_{int(step) - 1}"]
+            sent[f"{part}_{step}"] = call(kernel, [packet], [sums[part], held_now], 1)
+
+
 def solution(mesh):
+    n, count_x = mesh.shape["gz"], mesh.shape["gx"]
     in_specs = (P(("gx", "gy"), "gz"), P(), P(("gx", "gz"), "gy"))
     out_specs = P(("gx", "gz"), "gy")
-    return jax.shard_map(shards, mesh=mesh, in_specs=in_specs, out_specs=out_specs, check_vma=False)
+    if n != 4 or mesh.shape["gy"] != n or count_x < 2:
+        return jax.shard_map(plain, mesh=mesh, in_specs=in_specs, out_specs=out_specs, check_vma=False)
+
+    def body(panels, sizes, front):
+        return shards(n, count_x, panels, sizes, front)
+
+    return jax.shard_map(body, mesh=mesh, in_specs=in_specs, out_specs=out_specs, check_vma=False)

time: 190 us -> 104 us (0.55)
  the two profiles are of different devices: /device:TPU:0 before, /device:TPU:15 now
where the time goes in v1:
time: 104 us; the launch traced here: 103 us
  waiting for transfers between devices  42.8 us (41%)
  starting transfers between devices  39.4 us (38%)
  Pallas kernels  18.3 us (18%)
  local copies, waits for them, and re-layouts  1.42 us (1%)
    ppermute x20, waiting for transfers between devices, move(): return lax.ppermute(value, axes, pairs)  42.8 us
    ppermute x20, starting transfers between devices, move(): return lax.ppermute(value, axes, pairs)  39.4 us
    pallas_call x15, Pallas kernels, call(): pl.pallas_call(kernel, out_shape=outs if len(outs) > 1 else outs[0], in_s...  18.3 us
  transfers between devices with their start and end apart: 20, of which 6 were waited for; matrix products, arithmetic and copies ran while one was open for 1% of the time, Pallas kernels for 16%

profile of v1, /device:TPU:15, one launch (start us, length us, event | category | flops | bytes accessed | tf_op | source)
XLA Modules:
  0.0 103.1 jit_solution(12416864358244363708)
XLA Ops:
  0.7 3.3 %collective-permute-start.1 = (bf16[384,2048]{1,0:T(8,128)(2,1)}, bf16[384,2048]{1,0:T(8,128)(2,1)}, u32[]{:S(2)}, u32[]{:S(2)}) collective-permute-start(bf16[384,2048]{1,0:T(8,128)(2,1)} %panels.5), channel_id=1, source_target_pairs={{0,8},{12,4},{1,9},{13,5},{2,10},{14,6},{3,11},{15,7},{16,24},{28,... | collective-permute-start | bytes 4718600 | tf_op jit(solution)/shard_map/ppermute | solution.py:278
  4.0 3.3 %collective-permute-start.3 = (bf16[384,2048]{1,0:T(8,128)(2,1)S(1)}, bf16[384,2048]{1,0:T(8,128)(2,1)S(1)}, u32[]{:S(2)}, u32[]{:S(2)}) collective-permute-start(bf16[384,2048]{1,0:T(8,128)(2,1)S(1)} %collective-permute-done.beside), channel_id=1, source_target_pairs={{0,12},{12,0},{1,13},{13,1},{2,14},{14,2},{3,15},{15,3},{16,28},{2... | collective-permute-start | bytes 4718600 | tf_op jit(solution)/shard_map/ppermute | solution.py:278
  7.6 12.9 %collective-permute-done.1.first = bf16[384,2048]{1,0:T(8,128)(2,1)} collective-permute-done((bf16[384,2048]{1,0:T(8,128)(2,1)}, bf16[384,2048]{1,0:T(8,128)(2,1)}, u32[]{:S(2)}, u32[]{:S(2)}) %collective-permute-start.1) | collective-permute-done | bytes 1572896 | tf_op jit(solution)/shard_map/ppermute | solution.py:278
  21.8 18.0 %collective-permute-done.3.first = bf16[384,2048]{1,0:T(8,128)(2,1)S(1)} collective-permute-done((bf16[384,2048]{1,0:T(8,128)(2,1)S(1)}, bf16[384,2048]{1,0:T(8,128)(2,1)S(1)}, u32[]{:S(2)}, u32[]{:S(2)}) %collective-permute-start.3) | collective-permute-done | bytes 1572896 | tf_op jit(solution)/shard_map/ppermute | solution.py:278
  39.8 2.5 %collective-permute-start.4 = (bf16[384,2048]{1,0:T(8,128)(2,1)S(1)}, bf16[384,2048]{1,0:T(8,128)(2,1)}, u32[]{:S(2)}, u32[]{:S(2)}) collective-permute-start(bf16[384,2048]{1,0:T(8,128)(2,1)S(1)} %collective-permute-done.3.first), channel_id=1, source_target_pairs={{12,8},{0,4},{13,9},{1,5},{14,10},{2,6},{15,11},{3,7},{28,24},{16,... | collective-permute-start | bytes 4718600 | tf_op jit(solution)/shard_map/ppermute | solution.py:278
  43.2 1.4 %copy-done = bf16[384,2048]{1,0:T(8,128)(2,1)S(1)} copy-done((bf16[384,2048]{1,0:T(8,128)(2,1)S(1)}, bf16[384,2048]{1,0:T(8,128)(2,1)}, u32[]{:S(2)}) %copy-start) | copy-done | bytes 1572888
  44.6 2.0 %shard_map.37 = (f32[2,384,384]{2,1,0:T(8,128)S(1)}, s16[400,384]{1,0:T(8,128)(2,1)S(1)}) custom-call(bf16[1,2048]{1,0:T(2,128)(2,1)S(1)} %bitcast.4, bf16[384,2048]{1,0:T(8,128)(2,1)S(1)} %copy-done, bf16[384,2048]{1,0:T(8,128)(2,1)S(1)} %collective-permute-done.beside, bf16[384,2048]{1,0:T(8,128)(2,1)S(1)} %copy-done), custom_call_target="tpu_custom_call" | custom-call | flops 603979776 | bytes 6209536 | tf_op jit(solution)/shard_map/pallas_call | solution.py:170
  46.5 1.3 %collective-permute-start.6 = (s16[400,384]{1,0:T(8,128)(2,1)S(1)}, s16[400,384]{1,0:T(8,128)(2,1)S(1)}, u32[]{:S(2)}, u32[]{:S(2)}) collective-permute-start(s16[400,384]{1,0:T(8,128)(2,1)S(1)} %get-tuple-element.21), channel_id=1, source_target_pairs={{3,2},{0,1},{7,6},{4,5},{8,9},{11,10},{12,13},{15,14},{19,18},{16,... | collective-permute-start | bytes 921608 | tf_op jit(solution)/shard_map/ppermute | solution.py:278
  47.8 4.1 %shard_map.40 = (f32[2,384,384]{2,1,0:T(8,128)S(1)}, s16[400,384]{1,0:T(8,128)(2,1)S(1)}) custom-call(bf16[1,2048]{1,0:T(2,128)(2,1)S(1)} %bitcast.5, bf16[384,2048]{1,0:T(8,128)(2,1)S(1)} %copy-done.1, bf16[384,2048]{1,0:T(8,128)(2,1)S(1)} %collective-permute-done.beside, bf16[384,2048]{1,0:T(8,128)(2,1)} %collective-permute-done.1.first, ...), custom_call_target="tpu_custom_call" | custom-call | flops 1207959552 | bytes 9355264 | tf_op jit(solution)/shard_map/pallas_call | solution.py:170
  53.3 3.0 %shard_map.38 = (f32[384,384]{1,0:T(8,128)S(1)}, s16[400,384]{1,0:T(8,128)(2,1)S(1)}) custom-call(bf16[1,2048]{1,0:T(2,128)(2,1)S(1)} %bitcast.6, bf16[384,2048]{1,0:T(8,128)(2,1)} %collective-permute-done.1.first, bf16[384,2048]{1,0:T(8,128)(2,1)} %collective-permute-done.2.second, bf16[384,2048]{1,0:T(8,128)(2,1)S(1)} %copy-done.1), custom_call_target="tpu_custom_call" | custom-call | flops 603979776 | bytes 5619712 | tf_op jit(solution)/shard_map/pallas_call | solution.py:170
  57.9 3.0 %collective-permute-start.7 = (s16[400,384]{1,0:T(8,128)(2,1)S(1)}, s16[400,384]{1,0:T(8,128)(2,1)S(1)}, u32[]{:S(2)}, u32[]{:S(2)}) collective-permute-start(s16[400,384]{1,0:T(8,128)(2,1)S(1)} %shard_map.43), channel_id=1, source_target_pairs={{3,2},{2,1},{7,6},{6,5},{8,9},{9,10},{12,13},{13,14},{19,18},{18,1... | collective-permute-start | bytes 921608 | tf_op jit(solution)/shard_map/ppermute | solution.py:278
  60.9 2.4 %collective-permute-done.14.held = s16[400,384]{1,0:T(8,128)(2,1)S(1)} collective-permute-done((s16[400,384]{1,0:T(8,128)(2,1)S(1)}, s16[400,384]{1,0:T(8,128)(2,1)S(1)}, u32[]{:S(2)}, u32[]{:S(2)}) %collective-permute-start.14) | collective-permute-done | bytes 307232 | tf_op jit(solution)/shard_map/ppermute | solution.py:278
  63.6 3.2 %collective-permute-start.15 = (s16[400,384]{1,0:T(8,128)(2,1)S(1)}, s16[400,384]{1,0:T(8,128)(2,1)S(1)}, u32[]{:S(2)}, u32[]{:S(2)}) collective-permute-start(s16[400,384]{1,0:T(8,128)(2,1)S(1)} %shard_map.48), channel_id=1, source_target_pairs={{2,1},{6,5},{9,10},{13,14},{1,2},{5,6},{10,9},{14,13},{18,17},{22,... | collective-permute-start | bytes 921608 | tf_op jit(solution)/shard_map/ppermute | solution.py:278
  66.8 1.3 %collective-permute-start.10 = (s16[400,384]{1,0:T(8,128)(2,1)S(1)}, s16[400,384]{1,0:T(8,128)(2,1)S(1)}, u32[]{:S(2)}, u32[]{:S(2)}) collective-permute-start(s16[400,384]{1,0:T(8,128)(2,1)S(1)} %shard_map.45), channel_id=1, source_target_pairs={{1,2},{5,6},{10,9},{14,13},{17,18},{21,22},{26,25},{30,29}} | collective-permute-start | bytes 921608 | tf_op jit(solution)/shard_map/ppermute | solution.py:278
  68.1 3.7 %shard_map.41 = (f32[2,384,384]{2,1,0:T(8,128)S(1)}, s16[400,384]{1,0:T(8,128)(2,1)S(1)}, s16[400,384]{1,0:T(8,128)(2,1)S(1)}) custom-call(bf16[1,2048]{1,0:T(2,128)(2,1)S(1)} %bitcast.7, bf16[384,2048]{1,0:T(8,128)(2,1)S(1)} %copy-done.1, bf16[384,2048]{1,0:T(8,128)(2,1)S(1)} %collective-permute-done.beside, ...), custom_call_target="tpu_custom_call" | custom-call | flops 1207959552 | bytes 9662464 | tf_op jit(solution)/shard_map/pallas_call | solution.py:170
  73.1 2.5 %shard_map.39 = (f32[384,384]{1,0:T(8,128)S(1)}, s16[400,384]{1,0:T(8,128)(2,1)S(1)}) custom-call(bf16[1,2048]{1,0:T(2,128)(2,1)S(1)} %bitcast.8, bf16[384,2048]{1,0:T(8,128)(2,1)S(1)} %collective-permute-done.3.first, bf16[384,2048]{1,0:T(8,128)(2,1)} %collective-permute-done.4.second, bf16[384,2048]{1,0:T(8,128)(2,1)S(1)} %copy-done.1), custom_call_target="tpu_custom_call" | custom-call | flops 603979776 | bytes 5619712 | tf_op jit(solution)/shard_map/pallas_call | solution.py:170
  75.6 1.3 %collective-permute-start.12 = (s16[400,384]{1,0:T(8,128)(2,1)S(1)}, s16[400,384]{1,0:T(8,128)(2,1)S(1)}, u32[]{:S(2)}, u32[]{:S(2)}) collective-permute-start(s16[400,384]{1,0:T(8,128)(2,1)S(1)} %get-tuple-element.23), channel_id=1, source_target_pairs={{0,1},{3,2},{4,5},{7,6},{11,10},{8,9},{15,14},{12,13},{16,17},{19,... | collective-permute-start | bytes 921608 | tf_op jit(solution)/shard_map/ppermute | solution.py:278
  77.2 4.0 %collective-permute-start.8 = (s16[400,384]{1,0:T(8,128)(2,1)S(1)}, s16[400,384]{1,0:T(8,128)(2,1)S(1)}, u32[]{:S(2)}, u32[]{:S(2)}) collective-permute-start(s16[400,384]{1,0:T(8,128)(2,1)S(1)} %shard_map.44), channel_id=1, source_target_pairs={{2,1},{1,0},{6,5},{5,4},{9,10},{10,11},{13,14},{14,15},{18,17},{17... | collective-permute-start | bytes 921608 | tf_op jit(solution)/shard_map/ppermute | solution.py:278
  81.5 1.3 %collective-permute-start.16 = (s16[400,384]{1,0:T(8,128)(2,1)S(1)}, s16[400,384]{1,0:T(8,128)(2,1)S(1)}, u32[]{:S(2)}, u32[]{:S(2)}) collective-permute-start(s16[400,384]{1,0:T(8,128)(2,1)S(1)} %shard_map.49), channel_id=1, source_target_pairs={{1,0},{5,4},{10,11},{14,15},{2,3},{6,7},{9,8},{13,12},{17,16},{21,... | collective-permute-start | bytes 921608 | tf_op jit(solution)/shard_map/ppermute | solution.py:278
  83.0 1.4 %collective-permute-start.11 = (s16[400,384]{1,0:T(8,128)(2,1)S(1)}, s16[400,384]{1,0:T(8,128)(2,1)S(1)}, u32[]{:S(2)}, u32[]{:S(2)}) collective-permute-start(s16[400,384]{1,0:T(8,128)(2,1)S(1)} %shard_map.46), channel_id=1, source_target_pairs={{2,3},{6,7},{9,8},{13,12},{18,19},{22,23},{25,24},{29,28}} | collective-permute-start | bytes 921608 | tf_op jit(solution)/shard_map/ppermute | solution.py:278
  86.1 5.4 %collective-permute-start.18 = (s16[400,384]{1,0:T(8,128)(2,1)S(1)}, s16[400,384]{1,0:T(8,128)(2,1)S(1)}, u32[]{:S(2)}, u32[]{:S(2)}) collective-permute-start(s16[400,384]{1,0:T(8,128)(2,1)S(1)} %shard_map.50), channel_id=1, source_target_pairs={{2,1},{6,5},{9,10},{13,14},{1,2},{5,6},{10,9},{14,13},{18,17},{22,... | collective-permute-start | bytes 921608 | tf_op jit(solution)/shard_map/ppermute | solution.py:278
  93.1 5.4 %collective-permute-done.18.rest_6_ = s16[400,384]{1,0:T(8,128)(2,1)S(1)} collective-permute-done((s16[400,384]{1,0:T(8,128)(2,1)S(1)}, s16[400,384]{1,0:T(8,128)(2,1)S(1)}, u32[]{:S(2)}, u32[]{:S(2)}) %collective-permute-start.18) | collective-permute-done | bytes 307232 | tf_op jit(solution)/shard_map/ppermute | solution.py:278
  98.4 3.3 %collective-permute-done.13.rest_4_ = s16[400,384]{1,0:T(8,128)(2,1)S(1)} collective-permute-done((s16[400,384]{1,0:T(8,128)(2,1)S(1)}, s16[400,384]{1,0:T(8,128)(2,1)S(1)}, u32[]{:S(2)}, u32[]{:S(2)}) %collective-permute-start.13) | collective-permute-done | bytes 307232 | tf_op jit(solution)/shard_map/ppermute | solution.py:278
  101.7 1.4 %shard_map.51 = f32[384,768]{1,0:T(8,128)} custom-call(f32[384,768]{1,0:T(8,128)S(1)} %shard_map.42.base, s16[400,384]{1,0:T(8,128)(2,1)S(1)} %collective-permute-done.6.held.rest_0_, s16[400,384]{1,0:T(8,128)(2,1)S(1)} %collective-permute-done.8.rest_1_, s16[400,384]{1,0:T(8,128)(2,1)S(1)} %collective-permute-done.11.rest_2_, ...), custom_call_target="tpu_custom_call" | custom-call | flops 1 | bytes 4816896 | tf_op jit(solution)/shard_map/pallas_call | solution.py:170
  (41 shorter events, 11.5 us)
Async XLA Ops:
  0.0 4.0 %collective-permute-start = (bf16[384,2048]{1,0:T(8,128)(2,1)}, bf16[384,2048]{1,0:T(8,128)(2,1)S(1)}, u32[]{:S(2)}, u32[]{:S(2)}) collective-permute-start(bf16[384,2048]{1,0:T(8,128)(2,1)} %panels.5), channel_id=1, source_target_pairs={{0,4},{4,0},{8,12},{12,8},{1,5},{5,1},{9,13},{13,9},{2,6},{6,2},{1... | collective-permute-start | bytes 4718600 | tf_op jit(solution)/shard_map/ppermute | solution.py:278
  0.7 19.8 %collective-permute-start.1 = (bf16[384,2048]{1,0:T(8,128)(2,1)}, bf16[384,2048]{1,0:T(8,128)(2,1)}, u32[]{:S(2)}, u32[]{:S(2)}) collective-permute-start(bf16[384,2048]{1,0:T(8,128)(2,1)} %panels.5), channel_id=1, source_target_pairs={{0,8},{12,4},{1,9},{13,5},{2,10},{14,6},{3,11},{15,7},{16,24},{28,... | collective-permute-start | bytes 4718600 | tf_op jit(solution)/shard_map/ppermute | solution.py:278
  4.0 35.8 %collective-permute-start.3 = (bf16[384,2048]{1,0:T(8,128)(2,1)S(1)}, bf16[384,2048]{1,0:T(8,128)(2,1)S(1)}, u32[]{:S(2)}, u32[]{:S(2)}) collective-permute-start(bf16[384,2048]{1,0:T(8,128)(2,1)S(1)} %collective-permute-done.beside), channel_id=1, source_target_pairs={{0,12},{12,0},{1,13},{13,1},{2,14},{14,2},{3,15},{15,3},{16,28},{2... | collective-permute-start | bytes 4718600 | tf_op jit(solution)/shard_map/ppermute | solution.py:278
  7.3 40.6 %collective-permute-start.5 = (bf16[384,2048]{1,0:T(8,128)(2,1)}, bf16[384,2048]{1,0:T(8,128)(2,1)}, u32[]{:S(2)}, u32[]{:S(2)}) collective-permute-start(bf16[384,2048]{1,0:T(8,128)(2,1)} %panels.5), channel_id=1, source_target_pairs={{16,0},{0,16},{17,1},{1,17},{18,2},{2,18},{19,3},{3,19},{20,4},{4,... | collective-permute-start | bytes 4718600 | tf_op jit(solution)/shard_map/ppermute | solution.py:278
  20.5 27.4 %collective-permute-start.2 = (bf16[384,2048]{1,0:T(8,128)(2,1)}, bf16[384,2048]{1,0:T(8,128)(2,1)}, u32[]{:S(2)}, u32[]{:S(2)}) collective-permute-start(bf16[384,2048]{1,0:T(8,128)(2,1)} %collective-permute-done.1.first), channel_id=1, source_target_pairs={{8,12},{4,0},{9,13},{5,1},{10,14},{6,2},{11,15},{7,3},{24,28},{20,... | collective-permute-start | bytes 4718600 | tf_op jit(solution)/shard_map/ppermute | solution.py:278
  39.8 28.4 %collective-permute-start.4 = (bf16[384,2048]{1,0:T(8,128)(2,1)S(1)}, bf16[384,2048]{1,0:T(8,128)(2,1)}, u32[]{:S(2)}, u32[]{:S(2)}) collective-permute-start(bf16[384,2048]{1,0:T(8,128)(2,1)S(1)} %collective-permute-done.3.first), channel_id=1, source_target_pairs={{12,8},{0,4},{13,9},{1,5},{14,10},{2,6},{15,11},{3,7},{28,24},{16,... | collective-permute-start | bytes 4718600 | tf_op jit(solution)/shard_map/ppermute | solution.py:278
  43.1 1.4 %copy-start = (bf16[384,2048]{1,0:T(8,128)(2,1)S(1)}, bf16[384,2048]{1,0:T(8,128)(2,1)}, u32[]{:S(2)}) copy-start(bf16[384,2048]{1,0:T(8,128)(2,1)} %panels.5) | copy-start | bytes 4718596
  44.5 3.3 %copy-start.1 = (bf16[384,2048]{1,0:T(8,128)(2,1)S(1)}, bf16[384,2048]{1,0:T(8,128)(2,1)}, u32[]{:S(2)}) copy-start(bf16[384,2048]{1,0:T(8,128)(2,1)} %panels.5) | copy-start | bytes 4718596
  46.5 11.2 %collective-permute-start.6 = (s16[400,384]{1,0:T(8,128)(2,1)S(1)}, s16[400,384]{1,0:T(8,128)(2,1)S(1)}, u32[]{:S(2)}, u32[]{:S(2)}) collective-permute-start(s16[400,384]{1,0:T(8,128)(2,1)S(1)} %get-tuple-element.21), channel_id=1, source_target_pairs={{3,2},{0,1},{7,6},{4,5},{8,9},{11,10},{12,13},{15,14},{19,18},{16,... | collective-permute-start | bytes 921608 | tf_op jit(solution)/shard_map/ppermute | solution.py:278
  52.0 11.3 %collective-permute-start.14 = (s16[400,384]{1,0:T(8,128)(2,1)S(1)}, s16[400,384]{1,0:T(8,128)(2,1)S(1)}, u32[]{:S(2)}, u32[]{:S(2)}) collective-permute-start(s16[400,384]{1,0:T(8,128)(2,1)S(1)} %get-tuple-element.24), channel_id=1, source_target_pairs={{3,2},{7,6},{8,9},{12,13},{0,1},{4,5},{11,10},{15,14},{19,18},{23,... | collective-permute-start | bytes 921608 | tf_op jit(solution)/shard_map/ppermute | solution.py:278
  56.3 10.5 %collective-permute-start.9 = (s16[400,384]{1,0:T(8,128)(2,1)S(1)}, s16[400,384]{1,0:T(8,128)(2,1)S(1)}, u32[]{:S(2)}, u32[]{:S(2)}) collective-permute-start(s16[400,384]{1,0:T(8,128)(2,1)S(1)} %get-tuple-element.22), channel_id=1, source_target_pairs={{0,1},{4,5},{11,10},{15,14},{16,17},{20,21},{27,26},{31,30}} | collective-permute-start | bytes 921608 | tf_op jit(solution)/shard_map/ppermute | solution.py:278
  57.9 19.0 %collective-permute-start.7 = (s16[400,384]{1,0:T(8,128)(2,1)S(1)}, s16[400,384]{1,0:T(8,128)(2,1)S(1)}, u32[]{:S(2)}, u32[]{:S(2)}) collective-permute-start(s16[400,384]{1,0:T(8,128)(2,1)S(1)} %shard_map.43), channel_id=1, source_target_pairs={{3,2},{2,1},{7,6},{6,5},{8,9},{9,10},{12,13},{13,14},{19,18},{18,1... | collective-permute-start | bytes 921608 | tf_op jit(solution)/shard_map/ppermute | solution.py:278
  63.6 17.6 %collective-permute-start.15 = (s16[400,384]{1,0:T(8,128)(2,1)S(1)}, s16[400,384]{1,0:T(8,128)(2,1)S(1)}, u32[]{:S(2)}, u32[]{:S(2)}) collective-permute-start(s16[400,384]{1,0:T(8,128)(2,1)S(1)} %shard_map.48), channel_id=1, source_target_pairs={{2,1},{6,5},{9,10},{13,14},{1,2},{5,6},{10,9},{14,13},{18,17},{22,... | collective-permute-start | bytes 921608 | tf_op jit(solution)/shard_map/ppermute | solution.py:278
  66.8 16.0 %collective-permute-start.10 = (s16[400,384]{1,0:T(8,128)(2,1)S(1)}, s16[400,384]{1,0:T(8,128)(2,1)S(1)}, u32[]{:S(2)}, u32[]{:S(2)}) collective-permute-start(s16[400,384]{1,0:T(8,128)(2,1)S(1)} %shard_map.45), channel_id=1, source_target_pairs={{1,2},{5,6},{10,9},{14,13},{17,18},{21,22},{26,25},{30,29}} | collective-permute-start | bytes 921608 | tf_op jit(solution)/shard_map/ppermute | solution.py:278
  71.8 12.7 %collective-permute-start.17 = (s16[400,384]{1,0:T(8,128)(2,1)S(1)}, s16[400,384]{1,0:T(8,128)(2,1)S(1)}, u32[]{:S(2)}, u32[]{:S(2)}) collective-permute-start(s16[400,384]{1,0:T(8,128)(2,1)S(1)} %get-tuple-element.25), channel_id=1, source_target_pairs={{3,2},{7,6},{8,9},{12,13},{0,1},{4,5},{11,10},{15,14},{19,18},{23,... | collective-permute-start | bytes 921608 | tf_op jit(solution)/shard_map/ppermute | solution.py:278
  75.6 10.4 %collective-permute-start.12 = (s16[400,384]{1,0:T(8,128)(2,1)S(1)}, s16[400,384]{1,0:T(8,128)(2,1)S(1)}, u32[]{:S(2)}, u32[]{:S(2)}) collective-permute-start(s16[400,384]{1,0:T(8,128)(2,1)S(1)} %get-tuple-element.23), channel_id=1, source_target_pairs={{0,1},{3,2},{4,5},{7,6},{11,10},{8,9},{15,14},{12,13},{16,17},{19,... | collective-permute-start | bytes 921608 | tf_op jit(solution)/shard_map/ppermute | solution.py:278
  77.2 14.3 %collective-permute-start.8 = (s16[400,384]{1,0:T(8,128)(2,1)S(1)}, s16[400,384]{1,0:T(8,128)(2,1)S(1)}, u32[]{:S(2)}, u32[]{:S(2)}) collective-permute-start(s16[400,384]{1,0:T(8,128)(2,1)S(1)} %shard_map.44), channel_id=1, source_target_pairs={{2,1},{1,0},{6,5},{5,4},{9,10},{10,11},{13,14},{14,15},{18,17},{17... | collective-permute-start | bytes 921608 | tf_op jit(solution)/shard_map/ppermute | solution.py:278
  81.5 11.6 %collective-permute-start.16 = (s16[400,384]{1,0:T(8,128)(2,1)S(1)}, s16[400,384]{1,0:T(8,128)(2,1)S(1)}, u32[]{:S(2)}, u32[]{:S(2)}) collective-permute-start(s16[400,384]{1,0:T(8,128)(2,1)S(1)} %shard_map.49), channel_id=1, source_target_pairs={{1,0},{5,4},{10,11},{14,15},{2,3},{6,7},{9,8},{13,12},{17,16},{21,... | collective-permute-start | bytes 921608 | tf_op jit(solution)/shard_map/ppermute | solution.py:278
  83.0 9.8 %copy-start.2 = (f32[384,768]{1,0:T(8,128)S(1)}, f32[384,768]{1,0:T(8,128)}, u32[]{:S(2)}) copy-start(f32[384,768]{1,0:T(8,128)} %front.1) | copy-start | bytes 3538948
  83.0 10.0 %collective-permute-start.11 = (s16[400,384]{1,0:T(8,128)(2,1)S(1)}, s16[400,384]{1,0:T(8,128)(2,1)S(1)}, u32[]{:S(2)}, u32[]{:S(2)}) collective-permute-start(s16[400,384]{1,0:T(8,128)(2,1)S(1)} %shard_map.46), channel_id=1, source_target_pairs={{2,3},{6,7},{9,8},{13,12},{18,19},{22,23},{25,24},{29,28}} | collective-permute-start | bytes 921608 | tf_op jit(solution)/shard_map/ppermute | solution.py:278
  84.5 8.6 %collective-permute-start.19 = (s16[400,384]{1,0:T(8,128)(2,1)S(1)}, s16[400,384]{1,0:T(8,128)(2,1)S(1)}, u32[]{:S(2)}, u32[]{:S(2)}) collective-permute-start(s16[400,384]{1,0:T(8,128)(2,1)S(1)} %get-tuple-element.26), channel_id=1, source_target_pairs={{0,1},{4,5},{11,10},{15,14},{3,2},{7,6},{8,9},{12,13},{16,17},{20,... | collective-permute-start | bytes 921608 | tf_op jit(solution)/shard_map/ppermute | solution.py:278
  86.1 12.4 %collective-permute-start.18 = (s16[400,384]{1,0:T(8,128)(2,1)S(1)}, s16[400,384]{1,0:T(8,128)(2,1)S(1)}, u32[]{:S(2)}, u32[]{:S(2)}) collective-permute-start(s16[400,384]{1,0:T(8,128)(2,1)S(1)} %shard_map.50), channel_id=1, source_target_pairs={{2,1},{6,5},{9,10},{13,14},{1,2},{5,6},{10,9},{14,13},{18,17},{22,... | collective-permute-start | bytes 921608 | tf_op jit(solution)/shard_map/ppermute | solution.py:278
  91.5 10.2 %collective-permute-start.13 = (s16[400,384]{1,0:T(8,128)(2,1)S(1)}, s16[400,384]{1,0:T(8,128)(2,1)S(1)}, u32[]{:S(2)}, u32[]{:S(2)}) collective-permute-start(s16[400,384]{1,0:T(8,128)(2,1)S(1)} %shard_map.47), channel_id=1, source_target_pairs={{1,2},{5,6},{10,9},{14,13},{17,18},{21,22},{26,25},{30,29}} | collective-permute-start | bytes 921608 | tf_op jit(solution)/shard_map/ppermute | solution.py:278

commit v2 on v1

--- a/solution.py
+++ b/solution.py
@@ -10,7 +10,7 @@
 
 WIDTH = 1024
 GROUP = 64
-CODES = 16
+CODES = 8
 STEPS = 256.0
 TOP = 32767.0
 
@@ -52,10 +52,8 @@
     return g, w, far
 
 
-def product(rows, cols_ref, live_ref):
-    return lax.dot_general(
-        rows * live_ref[...], cols_ref[...], (((1,), (1,)), ((), ())), preferred_element_type=jnp.float32
-    )
+def product(rows, cols):
+    return lax.dot_general(rows, cols, (((1,), (1,)), ((), ())), preferred_element_type=jnp.float32)
 
 
 def decode(packet_ref, group, codes):
@@ -102,27 +100,34 @@
     return (g == 0) | (g == n - 1)
 
 
-def own_kernel(n, live, panels, beside, cols, sums, packet):
-    g, w, far = place(0, n)
-    sums[0] = product(panels[...], cols, live)
-    sums[1] = product(beside[...], cols, live)
-    at = jnp.where((g == far) == (w == 0), 0, 1)
+def own_kernel(n, live, panels, beside, cols, sums, locals_, packet):
+    _, w, _ = place(0, n)
+    ends = at_ends(n)
+    for index, pick in ((0, ends), (1, jnp.logical_not(ends))):
+        locals_[index] = jnp.where(pick, panels[...], beside[...]) * live[...]
+        sums[index] = product(locals_[index], cols[...])
+    at = jnp.where(w == 0, 0, 1)
     encode(packet, lambda group: sums[at, rows_of(group), :])
 
 
 def own_step_kernel(step, n, sums, held, packet):
-    g, w, far = place(0, n)
+    _, w, _ = place(0, n)
 
     @pl.when((w <= step) & (w >= step - 1))
     def _():
         codes = read_codes(held)
-        at = jnp.where((g == far) == (w == step), 0, 1)
+        at = jnp.where(w == step, 0, 1)
         encode(packet, lambda group: sums[at, rows_of(group), :] + decode(held, group, codes))
 
 
-def other_kernel(kind, n, live, first, second, cols, sums, packet):
-    pick = at_ends(n) == (kind == "near")
-    sums[...] = product(jnp.where(pick, first[...], second[...]), cols, live)
+def far_kernel(n, live, first, second, cols, sums, kept, packet):
+    kept[...] = jnp.where(at_ends(n), second[...], first[...]) * live[...]
+    sums[...] = product(kept[...], cols[...])
+    encode(packet, lambda group: sums[rows_of(group), :])
+
+
+def near_kernel(kept, cols, sums, packet):
+    sums[...] = product(kept[...], cols[...])
     encode(packet, lambda group: sums[rows_of(group), :])
 
 
@@ -135,20 +140,37 @@
         encode(packet, lambda group: sums[rows_of(group), :] + decode(held, group, codes))
 
 
-def both_kernel(kind, n, live, panels, beside, first, second, cols, sums, *packets):
-    z = lax.axis_index("gz")
-    ends = at_ends(n)
-    near = kind == "near"
-    top = n - 2 if near else n - 1
-    sums[0] = product(jnp.where(ends != near, panels[...], beside[...]), cols, live)
-    sums[1] = product(jnp.where(ends == near, first[...], second[...]), cols, live)
-    for index, packet in enumerate(packets):
-
-        @pl.when((z == 0) | (z == n - 1))
-        def _(index=index, packet=packet):
-            up = (z == 0) == (index == 0)
-            at = jnp.where(up, headed(top, n), headed(n - 1 - top, n))
-            encode(packet, lambda group: sums[at, rows_of(group), :])
+def both_far_kernel(n, locals_, kept, cols, sums, packet):
+    z = lax.axis_index("gz")
+    sums[0] = product(locals_[0], cols[...])
+    sums[1] = product(kept[...], cols[...])
+
+    @pl.when((z == 0) | (z == n - 1))
+    def _():
+        at = jnp.where(z == 0, headed(n - 1, n), headed(0, n))
+        encode(packet, lambda group: sums[at, rows_of(group), :])
+
+
+def both_near_kernel(n, makes, live, locals_, *rest):
+    if makes:
+        first, second, *cols, sums, packet, across, kept = rest
+        kept[...] = jnp.where(at_ends(n), first[...], second[...]) * live[...]
+    else:
+        kept, *cols, sums, packet, across = rest
+    z = lax.axis_index("gz")
+    start = 0
+    for part in cols:
+        at_columns = slice(start, start + part.shape[0])
+        sums[0, :, at_columns] = product(locals_[1], part[...])
+        sums[1, :, at_columns] = product(kept[...], part[...])
+        start += part.shape[0]
+
+    @pl.when((z == 0) | (z == n - 1))
+    def _():
+        low, high = headed(1, n), headed(n - 2, n)
+        on, off = jnp.where(z == 0, high, low), jnp.where(z == 0, low, high)
+        encode(packet, lambda group: sums[on, rows_of(group), :])
+        encode(across, lambda group: sums[off, rows_of(group), :])
 
 
 def both_step_kernel(kind, step, n, sums, held, packet):
@@ -177,19 +199,24 @@
     )(*operands)
 
 
-def base_kernel(n, count_x, front, *rest):
+def crossed_blocks(count_x, rows):
+    cut = rows
+    return [(d, at, min(cut, rows - at)) for d in range(1, count_x) for at in range(0, rows, cut)]
+
+
+def base_kernel(n, count_x, blocks, front, *rest):
     sums, out_ref = rest[:-1], rest[-1]
     x = lax.axis_index("gx")
     z = lax.axis_index("gz")
     rows = front.shape[0]
-    g, w, far = place(0, n)
-
-    def columns(d):
-        return pl.ds(pl.multiple_of(lax.rem(x + d, count_x) * rows, 128), rows)
+    _, w, _ = place(0, n)
+
+    def columns(d, at=0, size=rows):
+        return pl.ds(pl.multiple_of(lax.rem(x + d, count_x) * rows + at, 128), size)
 
     @pl.when(w >= n // 2)
     def _():
-        at = jnp.where((g == far) == (w == n - 1), 0, 1)
+        at = jnp.where(w == n - 1, 0, 1)
         out_ref[:, columns(0)] = front[:, columns(0)] - sums[0][at]
 
     for at_w, index in ((0, 1), (1, 2)):
@@ -199,24 +226,29 @@
             out_ref[:, columns(0)] = front[:, columns(0)] - sums[index][...]
 
     edge = (z == 0) | (z == n - 1)
-    for d in range(1, count_x):
-        for side, index in ((edge, 1 + 2 * d), (jnp.logical_not(edge), 2 + 2 * d)):
-
-            @pl.when(side)
-            def _(d=d, index=index):
-                mine = jnp.where(w >= n // 2, 0, 1)
-                out_ref[:, columns(d)] = front[:, columns(d)] - sums[index][mine]
-
-
-def final_kernel(n, count_x, base, *rest):
+    mine = jnp.where(w >= n // 2, 0, 1)
+
+    @pl.when(edge)
+    def _():
+        for index, place_of in enumerate(blocks):
+            out_ref[:, columns(*place_of)] = front[:, columns(*place_of)] - sums[3 + index][mine]
+
+    @pl.when(jnp.logical_not(edge))
+    def _():
+        for d in range(1, count_x):
+            out_ref[:, columns(d)] = front[:, columns(d)] - sums[2 + len(blocks) + d][mine]
+
+
+def final_kernel(n, count_x, blocks, base, *rest):
     packets, out_ref = rest[:-1], rest[-1]
     x = lax.axis_index("gx")
     z = lax.axis_index("gz")
     rows = base.shape[0]
     _, w, _ = place(0, n)
 
-    def finish(d, picks):
-        columns = pl.ds(pl.multiple_of(lax.rem(x + d, count_x) * rows, 128), rows)
+    def finish(place_of, picks):
+        d, at, size = place_of
+        columns = pl.ds(pl.multiple_of(lax.rem(x + d, count_x) * rows + at, 128), size)
         refs = [packets[k] for k in picks]
         codes = [read_codes(ref) for ref in refs]
         for group in range(rows // GROUP):
@@ -229,53 +261,64 @@
 
         @pl.when(w == at)
         def _(picks=picks):
-            finish(0, picks)
+            finish((0, 0, rows), picks)
 
     edge = (z == 0) | (z == n - 1)
-    for d in range(1, count_x):
-        for side, picks in ((edge, (2 + 3 * d,)), (jnp.logical_not(edge), (3 + 3 * d, 4 + 3 * d))):
-
-            @pl.when(side)
-            def _(d=d, picks=picks):
-                finish(d, picks)
-
-
-def plan(count_x):
+
+    @pl.when(edge)
+    def _():
+        for index, place_of in enumerate(blocks):
+            finish(place_of, (5 + index,))
+
+    @pl.when(jnp.logical_not(edge))
+    def _():
+        first = 5 + len(blocks)
+        for d in range(1, count_x):
+            finish((d, 0, rows), (first + 2 * d - 2, first + 2 * d - 1))
+
+
+def plan(count_x, blocks):
     crossed = range(1, count_x)
+    ends = range(1, blocks + 1)
 
     def go(label, step):
         return [f"{label}_k{step}", f">{label}_{step}"]
 
-    names = [">beside", ">far0"] + [f">cross{d}" for d in crossed] + [">near0"]
-    names += go("own", 0) + go("own", 1) + [">far1"] + go("far", 0) + go("own", 2)
-    for d in crossed:
-        names += go(f"xf{d}", 0)
-    names += [">near1"] + go("far", 1)
+    names = [">beside", ">far0"] + [f">cross{c}" for c in ends] + [">near0"]
+    names += go("own", 0) + go("own", 1) + [">far1"] + go("far", 0)
+    for c in ends:
+        if c == blocks:
+            names += go("own", 2) + [">near1"]
+        names += go(f"xf{c}", 0)
+    names += go("far", 1)
     for d in crossed:
         names += go(f"xn{d}", 0)
     names += go("near", 0)
     for d in crossed:
         names += [f">xn{d}_x"]
-    for d in crossed:
-        names += go(f"xf{d}", 1)
+    for c in ends:
+        names += go(f"xf{c}", 1)
     names += go("far", 2)
     for d in crossed:
         names += go(f"xn{d}", 1)
-    for d in crossed:
-        names += go(f"xf{d}", 2)
+    for c in ends:
+        names += go(f"xf{c}", 2)
     return names + go("near", 1) + ["base", "final"]
 
 
 def shards(n, count_x, panels, sizes, front):
     rows, width = panels.shape
     square = 2 * rows * rows * width
-    sums1 = jax.ShapeDtypeStruct((rows, rows), jnp.float32)
-    sums2 = jax.ShapeDtypeStruct((2, rows, rows), jnp.float32)
-    packet = jax.ShapeDtypeStruct((rows + CODES, rows), jnp.int16)
+    one_sum = jax.ShapeDtypeStruct((rows, rows), jnp.float32)
+    piece_like = jax.ShapeDtypeStruct((rows, width), jnp.bfloat16)
+
+    def pair_of_sums(size):
+        return jax.ShapeDtypeStruct((2, rows, size), jnp.float32)
+
+    def packet(size):
+        return jax.ShapeDtypeStruct((rows + CODES, size), jnp.int16)
+
     block = jax.ShapeDtypeStruct(front.shape, jnp.float32)
-
-    def move(value, axes, pairs):
-        return lax.ppermute(value, axes, pairs)
 
     def way(rnd, hops):
         pairs = []
@@ -317,48 +360,35 @@
         "far1": ("far0", [(2, 3), (1, 0)]),
         "near1": ("near0", [(3, 2), (0, 1)]),
     }
+    blocks = crossed_blocks(count_x, rows)
     held = {}
     sums = {}
     sent = {}
     got = {}
-    for name in plan(count_x):
+    for name in plan(count_x, len(blocks)):
         label = name.lstrip(">")
         part, _, step = label.partition("_")
         step = step.lstrip("k")
-        kind, d = part.rstrip("0123456789"), int("0" + part.lstrip("abcdefghijklmnopqrstuvwxyz"))
+        kind, c = part.rstrip("0123456789"), int("0" + part.lstrip("abcdefghijklmnopqrstuvwxyz"))
         if label in y_moves:
             source, pairs = y_moves[label]
-            held[label] = move(panels if source is None else held[source], "gy", pairs)
+            held[label] = lax.ppermute(panels if source is None else held[source], "gy", pairs)
         elif kind == "cross":
-            held[label] = move(panels, "gx", [((i + d) % count_x, i) for i in range(count_x)])
+            d, at, size = blocks[c - 1]
+            piece = panels if size == rows else lax.slice_in_dim(panels, at, at + size, axis=0)
+            held[label] = lax.ppermute(piece, "gx", [((i + d) % count_x, i) for i in range(count_x)])
         elif name[0] == ">":
-            got[label] = move(sent[label], ("gy", "gz"), hops[f"{kind}_{step}"])
+            got[label] = lax.ppermute(sent[label], ("gy", "gz"), hops[f"{kind}_{step}"])
         elif label == "base":
             each = [sums[k] for k in ("own", "far", "near")]
-            each += [sums[f"{k}{d}"] for d in range(1, count_x) for k in ("xf", "xn")]
-            base = call(functools.partial(base_kernel, n, count_x), [block], [front, *each], 1)
+            each += [sums[f"xf{c + 1}"] for c in range(len(blocks))] + [sums[f"xn{d}"] for d in range(1, count_x)]
+            base = call(functools.partial(base_kernel, n, count_x, blocks), [block], [front, *each], 1)
         elif label == "final":
             each = [got[k] for k in ("own_0", "own_2", "far_2", "near_0", "near_1")]
-            for d in range(1, count_x):
-                each += [got[f"xf{d}_2"], got[f"xn{d}_1"], got[f"xn{d}_x"]]
-            return call(functools.partial(final_kernel, n, count_x), [block], [base, *each], 1)
-        elif step == "0":
-            cols = held[f"cross{d}"] if d else panels
-            local = (panels, held["beside"])
-            other = () if kind == "own" else (held["far0"], held["far1"])
-            if kind in ("near", "xn"):
-                other = (held["near0"], held["near1"])
-            if kind == "own":
-                kernel, pieces, outs = functools.partial(own_kernel, n), local, [sums2, packet]
-            elif kind in ("far", "near"):
-                kernel, pieces, outs = functools.partial(other_kernel, kind, n), other, [sums1, packet]
-            else:
-                kernel = functools.partial(both_kernel, "far" if kind == "xf" else "near", n)
-                pieces, outs = (*local, *other), [sums2, packet] + [packet] * (kind == "xn")
-            done = call(kernel, outs, [live, *pieces, cols], len(pieces) * square // 2)
-            sums[part], sent[f"{part}_0"] = done[:2]
-            sent[f"{part}_x"] = done[-1]
-        else:
+            each += [got[f"xf{c + 1}_2"] for c in range(len(blocks))]
+            each += [got[f"xn{d}_{k}"] for d in range(1, count_x) for k in ("1", "x")]
+            return call(functools.partial(final_kernel, n, count_x, blocks), [block], [base, *each], 1)
+        elif step != "0":
             kernel = {
                 "own": functools.partial(own_step_kernel, int(step), n),
                 "far": functools.partial(other_step_kernel, int(step), n),
@@ -366,8 +396,45 @@
                 "xf": functools.partial(both_step_kernel, "far", int(step), n),
                 "xn": functools.partial(both_step_kernel, "near", int(step), n),
             }[kind]
-            held_now = got[f"{part}_{int(step) - 1}"]
-            sent[f"{part}_{step}"] = call(kernel, [packet], [sums[part], held_now], 1)
+            before = got[f"{part}_{int(step) - 1}"]
+            sent[f"{part}_{step}"] = call(kernel, [packet(before.shape[1])], [sums[part], before], 1)
+        elif kind == "own":
+            sums[part], held["locals"], sent["own_0"] = call(
+                functools.partial(own_kernel, n),
+                [pair_of_sums(rows), jax.ShapeDtypeStruct((2, rows, width), jnp.bfloat16), packet(rows)],
+                [live, panels, held["beside"], panels],
+                2 * square,
+            )
+        elif kind == "far":
+            sums[part], held["kept_far"], sent["far_0"] = call(
+                functools.partial(far_kernel, n),
+                [one_sum, piece_like, packet(rows)],
+                [live, held["far0"], held["far1"], panels],
+                square,
+            )
+        elif kind == "near":
+            sums[part], sent["near_0"] = call(near_kernel, [one_sum, packet(rows)], [held["kept_near"], panels], square)
+        elif kind == "xf":
+            size = blocks[c - 1][2]
+            sums[part], sent[f"{part}_0"] = call(
+                functools.partial(both_far_kernel, n),
+                [pair_of_sums(size), packet(size)],
+                [held["locals"], held["kept_far"], held[f"cross{c}"]],
+                4 * rows * size * width,
+            )
+        else:
+            makes = "kept_near" not in held
+            pieces = (held["near0"], held["near1"]) if makes else (held["kept_near"],)
+            cols = [held[f"cross{i + 1}"] for i, block_of in enumerate(blocks) if block_of[0] == c]
+            done = call(
+                functools.partial(both_near_kernel, n, makes),
+                [pair_of_sums(rows), packet(rows), packet(rows)] + [piece_like] * makes,
+                [live, held["locals"], *pieces, *cols],
+                2 * square,
+            )
+            sums[part], sent[f"{part}_0"], sent[f"{part}_x"] = done[:3]
+            if makes:
+                held["kept_near"] = done[3]
 
 
 def solution(mesh):

time: 104 us -> 119 us (1.14)
  the two profiles are of different devices: /device:TPU:15 before, /device:TPU:16 now
where the time goes in v2:
time: 119 us
  waiting for transfers between devices  56.5 us (47%)
  starting transfers between devices  43.1 us (36%)
  Pallas kernels  14 us (12%)
  local copies, waits for them, and re-layouts  4.02 us (3%)
    ppermute x14, starting transfers between devices, shards(): got[label] = lax.ppermute(sent[label], ('gy', 'gz'), hops[f'{kind}_{step}'])  31 us
    ppermute x5, waiting for transfers between devices, shards(): lax.ppermute(panels if source is None else held[source], 'gy', pairs)  28 us
    ppermute x14, waiting for transfers between devices, shards(): got[label] = lax.ppermute(sent[label], ('gy', 'gz'), hops[f'{kind}_{step}'])  20.6 us
    pallas_call x15, Pallas kernels, call(): pl.pallas_call(kernel, out_shape=outs if len(outs) > 1 else outs[0], in_s...  14 us
    ppermute x5, starting transfers between devices, shards(): lax.ppermute(panels if source is None else held[source], 'gy', pairs)  10.6 us
    ppermute x1, waiting for transfers between devices, shards(): lax.ppermute(piece, 'gx', [((i + d) % count_x, i) for i in range(count_x)])  7.84 us
    unnamed x11, local copies, waits for them, and re-layouts  4.02 us
  transfers between devices with their start and end apart: 20, of which 7 were waited for; matrix products, arithmetic and copies ran while one was open for 1% of the time, Pallas kernels for 11%

profile of v2, /device:TPU:16, one launch (start us, length us, event | category | flops | bytes accessed | tf_op | source)
XLA Modules:
  0.0 118.9 jit_solution(13137918344602161840)
XLA Ops:
  0.0 4.6 %collective-permute-start.1 = (bf16[384,2048]{1,0:T(8,128)(2,1)}, bf16[384,2048]{1,0:T(8,128)(2,1)}, u32[]{:S(2)}, u32[]{:S(2)}) collective-permute-start(bf16[384,2048]{1,0:T(8,128)(2,1)} %cols.5), channel_id=1, source_target_pairs={{0,8},{12,4},{1,9},{13,5},{2,10},{14,6},{3,11},{15,7},{16,24},{28,... | collective-permute-start | bytes 4718600 | tf_op jit(solution)/shard_map/ppermute | solution.py:375
  4.6 2.2 %collective-permute-start.3 = (bf16[384,2048]{1,0:T(8,128)(2,1)S(1)}, bf16[384,2048]{1,0:T(8,128)(2,1)S(1)}, u32[]{:S(2)}, u32[]{:S(2)}) collective-permute-start(bf16[384,2048]{1,0:T(8,128)(2,1)S(1)} %collective-permute-done.beside), channel_id=1, source_target_pairs={{0,12},{12,0},{1,13},{13,1},{2,14},{14,2},{3,15},{15,3},{16,28},{2... | collective-permute-start | bytes 4718600 | tf_op jit(solution)/shard_map/ppermute | solution.py:375
  8.1 13.6 %collective-permute-done.1.first = bf16[384,2048]{1,0:T(8,128)(2,1)} collective-permute-done((bf16[384,2048]{1,0:T(8,128)(2,1)}, bf16[384,2048]{1,0:T(8,128)(2,1)}, u32[]{:S(2)}, u32[]{:S(2)}) %collective-permute-start.1) | collective-permute-done | bytes 1572896 | tf_op jit(solution)/shard_map/ppermute | solution.py:375
  22.9 1.6 %collective-permute-start.5 = (bf16[384,2048]{1,0:T(8,128)(2,1)}, bf16[384,2048]{1,0:T(8,128)(2,1)S(1)}, u32[]{:S(2)}, u32[]{:S(2)}) collective-permute-start(bf16[384,2048]{1,0:T(8,128)(2,1)} %cols.5), channel_id=1, source_target_pairs={{16,0},{0,16},{17,1},{1,17},{18,2},{2,18},{19,3},{3,19},{20,4},{4,... | collective-permute-start | bytes 4718600 | tf_op jit(solution)/shard_map/ppermute | solution.py:379
  24.5 14.4 %collective-permute-done.3.rest_0_ = bf16[384,2048]{1,0:T(8,128)(2,1)S(1)} collective-permute-done((bf16[384,2048]{1,0:T(8,128)(2,1)S(1)}, bf16[384,2048]{1,0:T(8,128)(2,1)S(1)}, u32[]{:S(2)}, u32[]{:S(2)}) %collective-permute-start.3) | collective-permute-done | bytes 1572896 | tf_op jit(solution)/shard_map/ppermute | solution.py:375
  38.9 2.5 %collective-permute-start.4 = (bf16[384,2048]{1,0:T(8,128)(2,1)S(1)}, bf16[384,2048]{1,0:T(8,128)(2,1)}, u32[]{:S(2)}, u32[]{:S(2)}) collective-permute-start(bf16[384,2048]{1,0:T(8,128)(2,1)S(1)} %collective-permute-done.3.rest_0_), channel_id=1, source_target_pairs={{12,8},{0,4},{13,9},{1,5},{14,10},{2,6},{15,11},{3,7},{28,24},{16,... | collective-permute-start | bytes 4718600 | tf_op jit(solution)/shard_map/ppermute | solution.py:375
  42.3 1.4 %copy-done = bf16[384,2048]{1,0:T(8,128)(2,1)S(1)} copy-done((bf16[384,2048]{1,0:T(8,128)(2,1)S(1)}, bf16[384,2048]{1,0:T(8,128)(2,1)}, u32[]{:S(2)}) %copy-start) | copy-done | bytes 1572888
  43.7 1.4 %copy-done.3 = bf16[384,2048]{1,0:T(8,128)(2,1)S(1)} copy-done((bf16[384,2048]{1,0:T(8,128)(2,1)S(1)}, bf16[384,2048]{1,0:T(8,128)(2,1)}, u32[]{:S(2)}) %copy-start.3) | copy-done | bytes 1572888
  45.1 2.0 %shard_map.37 = (f32[2,384,384]{2,1,0:T(8,128)S(1)}, bf16[2,384,2048]{2,1,0:T(8,128)(2,1)S(1)}, s16[392,384]{1,0:T(8,128)(2,1)S(1)}) custom-call(bf16[1,2048]{1,0:T(2,128)(2,1)S(1)} %bitcast.4, bf16[384,2048]{1,0:T(8,128)(2,1)S(1)} %copy-done, bf16[384,2048]{1,0:T(8,128)(2,1)S(1)} %copy-done.3, bf16[384,2048]{1,0:T(8,128)(2,1)S(1)} %copy-done), custom_call_target="tpu_custom_call" | custom-call | flops 1207959552 | bytes 9349120 | tf_op jit(solution)/shard_map/pallas_call | solution.py:192
  48.4 3.0 %shard_map.38 = (f32[384,384]{1,0:T(8,128)S(1)}, bf16[384,2048]{1,0:T(8,128)(2,1)S(1)}, s16[392,384]{1,0:T(8,128)(2,1)S(1)}) custom-call(bf16[1,2048]{1,0:T(2,128)(2,1)S(1)} %bitcast.5, bf16[384,2048]{1,0:T(8,128)(2,1)} %collective-permute-done.1.first, bf16[384,2048]{1,0:T(8,128)(2,1)} %collective-permute-done.2.second, bf16[384,2048]{1,0:T(8,128)(2,1)S(1)} %copy-done.1), custom_call_target="tpu_custom_call" | custom-call | flops 603979776 | bytes 7186432 | tf_op jit(solution)/shard_map/pallas_call | solution.py:192
  51.4 7.8 %collective-permute-done.5.rest_2_.cols = bf16[384,2048]{1,0:T(8,128)(2,1)S(1)} collective-permute-done((bf16[384,2048]{1,0:T(8,128)(2,1)}, bf16[384,2048]{1,0:T(8,128)(2,1)S(1)}, u32[]{:S(2)}, u32[]{:S(2)}) %collective-permute-start.5) | collective-permute-done | bytes 1572896 | tf_op jit(solution)/shard_map/ppermute | solution.py:379
  59.2 1.8 %shard_map.41 = (f32[2,384,384]{2,1,0:T(8,128)S(1)}, s16[392,384]{1,0:T(8,128)(2,1)S(1)}) custom-call(bf16[2,384,2048]{2,1,0:T(8,128)(2,1)S(1)} %get-tuple-element.21.locals_, bf16[384,2048]{1,0:T(8,128)(2,1)S(1)} %get-tuple-element.24.kept, bf16[384,2048]{1,0:T(8,128)(2,1)S(1)} %collective-permute-done.5.rest_2_.cols), custom_call_target="tpu_custom_call" | custom-call | flops 1207959552 | bytes 7772160 | tf_op jit(solution)/shard_map/pallas_call | solution.py:192
  63.3 2.7 %collective-permute-start.7 = (s16[392,384]{1,0:T(8,128)(2,1)S(1)}, s16[392,384]{1,0:T(8,128)(2,1)S(1)}, u32[]{:S(2)}, u32[]{:S(2)}) collective-permute-start(s16[392,384]{1,0:T(8,128)(2,1)S(1)} %shard_map.43), channel_id=1, source_target_pairs={{3,2},{2,1},{7,6},{6,5},{8,9},{9,10},{12,13},{13,14},{19,18},{18,1... | collective-permute-start | bytes 903176 | tf_op jit(solution)/shard_map/ppermute | solution.py:381
  66.1 6.8 %collective-permute-done.14.held = s16[392,384]{1,0:T(8,128)(2,1)S(1)} collective-permute-done((s16[392,384]{1,0:T(8,128)(2,1)S(1)}, s16[392,384]{1,0:T(8,128)(2,1)S(1)}, u32[]{:S(2)}, u32[]{:S(2)}) %collective-permute-start.14) | collective-permute-done | bytes 301088 | tf_op jit(solution)/shard_map/ppermute | solution.py:381
  73.1 2.4 %collective-permute-start.15 = (s16[392,384]{1,0:T(8,128)(2,1)S(1)}, s16[392,384]{1,0:T(8,128)(2,1)S(1)}, u32[]{:S(2)}, u32[]{:S(2)}) collective-permute-start(s16[392,384]{1,0:T(8,128)(2,1)S(1)} %shard_map.48), channel_id=1, source_target_pairs={{2,1},{6,5},{9,10},{13,14},{1,2},{5,6},{10,9},{14,13},{18,17},{22,... | collective-permute-start | bytes 903176 | tf_op jit(solution)/shard_map/ppermute | solution.py:381
  76.8 3.2 %shard_map.39 = (f32[2,384,384]{2,1,0:T(8,128)S(1)}, s16[392,384]{1,0:T(8,128)(2,1)S(1)}, s16[392,384]{1,0:T(8,128)(2,1)S(1)}, bf16[384,2048]{1,0:T(8,128)(2,1)S(1)}) custom-call(bf16[1,2048]{1,0:T(2,128)(2,1)S(1)} %bitcast.6, bf16[2,384,2048]{2,1,0:T(8,128)(2,1)S(1)} %get-tuple-element.21.locals_, bf16[384,2048]{1,0:T(8,128)(2,1)S(1)} %collective-permute-done.3.rest_0_, ...), custom_call_target="tpu_custom_call" | custom-call | flops 1207959552 | bytes 11223040 | tf_op jit(solution)/shard_map/pallas_call | solution.py:192
  83.9 6.4 %collective-permute-start.8 = (s16[392,384]{1,0:T(8,128)(2,1)S(1)}, s16[392,384]{1,0:T(8,128)(2,1)S(1)}, u32[]{:S(2)}, u32[]{:S(2)}) collective-permute-start(s16[392,384]{1,0:T(8,128)(2,1)S(1)} %shard_map.44), channel_id=1, source_target_pairs={{2,1},{1,0},{6,5},{5,4},{9,10},{10,11},{13,14},{14,15},{18,17},{17... | collective-permute-start | bytes 903176 | tf_op jit(solution)/shard_map/ppermute | solution.py:381
  90.6 1.3 %collective-permute-start.16 = (s16[392,384]{1,0:T(8,128)(2,1)S(1)}, s16[392,384]{1,0:T(8,128)(2,1)S(1)}, u32[]{:S(2)}, u32[]{:S(2)}) collective-permute-start(s16[392,384]{1,0:T(8,128)(2,1)S(1)} %shard_map.49), channel_id=1, source_target_pairs={{1,0},{5,4},{10,11},{14,15},{2,3},{6,7},{9,8},{13,12},{17,16},{21,... | collective-permute-start | bytes 903176 | tf_op jit(solution)/shard_map/ppermute | solution.py:381
  92.2 1.4 %collective-permute-start.11 = (s16[392,384]{1,0:T(8,128)(2,1)S(1)}, s16[392,384]{1,0:T(8,128)(2,1)S(1)}, u32[]{:S(2)}, u32[]{:S(2)}) collective-permute-start(s16[392,384]{1,0:T(8,128)(2,1)S(1)} %shard_map.46), channel_id=1, source_target_pairs={{2,3},{6,7},{9,8},{13,12},{18,19},{22,23},{25,24},{29,28}} | collective-permute-start | bytes 903176 | tf_op jit(solution)/shard_map/ppermute | solution.py:381
  95.0 3.9 %collective-permute-done.17.held = s16[392,384]{1,0:T(8,128)(2,1)S(1)} collective-permute-done((s16[392,384]{1,0:T(8,128)(2,1)S(1)}, s16[392,384]{1,0:T(8,128)(2,1)S(1)}, u32[]{:S(2)}, u32[]{:S(2)}) %collective-permute-start.17) | collective-permute-done | bytes 301088 | tf_op jit(solution)/shard_map/ppermute | solution.py:381
  100.4 7.0 %collective-permute-start.18 = (s16[392,384]{1,0:T(8,128)(2,1)S(1)}, s16[392,384]{1,0:T(8,128)(2,1)S(1)}, u32[]{:S(2)}, u32[]{:S(2)}) collective-permute-start(s16[392,384]{1,0:T(8,128)(2,1)S(1)} %shard_map.50), channel_id=1, source_target_pairs={{2,1},{6,5},{9,10},{13,14},{1,2},{5,6},{10,9},{14,13},{18,17},{22,... | collective-permute-start | bytes 903176 | tf_op jit(solution)/shard_map/ppermute | solution.py:381
  107.7 5.5 %collective-permute-done.13.rest_4_ = s16[392,384]{1,0:T(8,128)(2,1)S(1)} collective-permute-done((s16[392,384]{1,0:T(8,128)(2,1)S(1)}, s16[392,384]{1,0:T(8,128)(2,1)S(1)}, u32[]{:S(2)}, u32[]{:S(2)}) %collective-permute-start.13) | collective-permute-done | bytes 301088 | tf_op jit(solution)/shard_map/ppermute | solution.py:381
  113.2 4.4 %collective-permute-done.18.rest_6_ = s16[392,384]{1,0:T(8,128)(2,1)S(1)} collective-permute-done((s16[392,384]{1,0:T(8,128)(2,1)S(1)}, s16[392,384]{1,0:T(8,128)(2,1)S(1)}, u32[]{:S(2)}, u32[]{:S(2)}) %collective-permute-start.18) | collective-permute-done | bytes 301088 | tf_op jit(solution)/shard_map/ppermute | solution.py:381
  117.6 1.4 %shard_map.51 = f32[384,768]{1,0:T(8,128)} custom-call(f32[384,768]{1,0:T(8,128)S(1)} %shard_map.42.base, s16[392,384]{1,0:T(8,128)(2,1)S(1)} %collective-permute-done.6.held.rest_0_, s16[392,384]{1,0:T(8,128)(2,1)S(1)} %collective-permute-done.8.rest_1_, s16[392,384]{1,0:T(8,128)(2,1)S(1)} %collective-permute-done.11.rest_2_, ...), custom_call_target="tpu_custom_call" | custom-call | flops 1 | bytes 4767744 | tf_op jit(solution)/shard_map/pallas_call | solution.py:192
  (45 shorter events, 15.9 us)
Async XLA Ops:
  0.0 4.6 %collective-permute-start = (bf16[384,2048]{1,0:T(8,128)(2,1)}, bf16[384,2048]{1,0:T(8,128)(2,1)S(1)}, u32[]{:S(2)}, u32[]{:S(2)}) collective-permute-start(bf16[384,2048]{1,0:T(8,128)(2,1)} %cols.5), channel_id=1, source_target_pairs={{0,4},{4,0},{8,12},{12,8},{1,5},{5,1},{9,13},{13,9},{2,6},{6,2},{1... | collective-permute-start | bytes 4718600 | tf_op jit(solution)/shard_map/ppermute | solution.py:375
  0.0 21.7 %collective-permute-start.1 = (bf16[384,2048]{1,0:T(8,128)(2,1)}, bf16[384,2048]{1,0:T(8,128)(2,1)}, u32[]{:S(2)}, u32[]{:S(2)}) collective-permute-start(bf16[384,2048]{1,0:T(8,128)(2,1)} %cols.5), channel_id=1, source_target_pairs={{0,8},{12,4},{1,9},{13,5},{2,10},{14,6},{3,11},{15,7},{16,24},{28,... | collective-permute-start | bytes 4718600 | tf_op jit(solution)/shard_map/ppermute | solution.py:375
  4.6 34.3 %collective-permute-start.3 = (bf16[384,2048]{1,0:T(8,128)(2,1)S(1)}, bf16[384,2048]{1,0:T(8,128)(2,1)S(1)}, u32[]{:S(2)}, u32[]{:S(2)}) collective-permute-start(bf16[384,2048]{1,0:T(8,128)(2,1)S(1)} %collective-permute-done.beside), channel_id=1, source_target_pairs={{0,12},{12,0},{1,13},{13,1},{2,14},{14,2},{3,15},{15,3},{16,28},{2... | collective-permute-start | bytes 4718600 | tf_op jit(solution)/shard_map/ppermute | solution.py:375
  21.7 26.8 %collective-permute-start.2 = (bf16[384,2048]{1,0:T(8,128)(2,1)}, bf16[384,2048]{1,0:T(8,128)(2,1)}, u32[]{:S(2)}, u32[]{:S(2)}) collective-permute-start(bf16[384,2048]{1,0:T(8,128)(2,1)} %collective-permute-done.1.first), channel_id=1, source_target_pairs={{8,12},{4,0},{9,13},{5,1},{10,14},{6,2},{11,15},{7,3},{24,28},{20,... | collective-permute-start | bytes 4718600 | tf_op jit(solution)/shard_map/ppermute | solution.py:375
  22.9 36.3 %collective-permute-start.5 = (bf16[384,2048]{1,0:T(8,128)(2,1)}, bf16[384,2048]{1,0:T(8,128)(2,1)S(1)}, u32[]{:S(2)}, u32[]{:S(2)}) collective-permute-start(bf16[384,2048]{1,0:T(8,128)(2,1)} %cols.5), channel_id=1, source_target_pairs={{16,0},{0,16},{17,1},{1,17},{18,2},{2,18},{19,3},{3,19},{20,4},{4,... | collective-permute-start | bytes 4718600 | tf_op jit(solution)/shard_map/ppermute | solution.py:379
  38.9 37.9 %collective-permute-start.4 = (bf16[384,2048]{1,0:T(8,128)(2,1)S(1)}, bf16[384,2048]{1,0:T(8,128)(2,1)}, u32[]{:S(2)}, u32[]{:S(2)}) collective-permute-start(bf16[384,2048]{1,0:T(8,128)(2,1)S(1)} %collective-permute-done.3.rest_0_), channel_id=1, source_target_pairs={{12,8},{0,4},{13,9},{1,5},{14,10},{2,6},{15,11},{3,7},{28,24},{16,... | collective-permute-start | bytes 4718600 | tf_op jit(solution)/shard_map/ppermute | solution.py:375
  42.3 1.4 %copy-start = (bf16[384,2048]{1,0:T(8,128)(2,1)S(1)}, bf16[384,2048]{1,0:T(8,128)(2,1)}, u32[]{:S(2)}) copy-start(bf16[384,2048]{1,0:T(8,128)(2,1)} %cols.5) | copy-start | bytes 4718596
  43.7 1.4 %copy-start.3 = (bf16[384,2048]{1,0:T(8,128)(2,1)S(1)}, bf16[384,2048]{1,0:T(8,128)(2,1)}, u32[]{:S(2)}) copy-start(bf16[384,2048]{1,0:T(8,128)(2,1)} %copy-done.2) | copy-start | bytes 4718596
  45.1 3.3 %copy-start.1 = (bf16[384,2048]{1,0:T(8,128)(2,1)S(1)}, bf16[384,2048]{1,0:T(8,128)(2,1)}, u32[]{:S(2)}) copy-start(bf16[384,2048]{1,0:T(8,128)(2,1)} %cols.5) | copy-start | bytes 4718596
  47.1 15.9 %collective-permute-start.6 = (s16[392,384]{1,0:T(8,128)(2,1)S(1)}, s16[392,384]{1,0:T(8,128)(2,1)S(1)}, u32[]{:S(2)}, u32[]{:S(2)}) collective-permute-start(s16[392,384]{1,0:T(8,128)(2,1)S(1)} %get-tuple-element.27), channel_id=1, source_target_pairs={{3,2},{0,1},{7,6},{4,5},{8,9},{11,10},{12,13},{15,14},{19,18},{16,... | collective-permute-start | bytes 903176 | tf_op jit(solution)/shard_map/ppermute | solution.py:381
  61.0 11.8 %collective-permute-start.14 = (s16[392,384]{1,0:T(8,128)(2,1)S(1)}, s16[392,384]{1,0:T(8,128)(2,1)S(1)}, u32[]{:S(2)}, u32[]{:S(2)}) collective-permute-start(s16[392,384]{1,0:T(8,128)(2,1)S(1)} %get-tuple-element.30), channel_id=1, source_target_pairs={{3,2},{7,6},{8,9},{12,13},{0,1},{4,5},{11,10},{15,14},{19,18},{23,... | collective-permute-start | bytes 903176 | tf_op jit(solution)/shard_map/ppermute | solution.py:381
  62.3 13.1 %collective-permute-start.9 = (s16[392,384]{1,0:T(8,128)(2,1)S(1)}, s16[392,384]{1,0:T(8,128)(2,1)S(1)}, u32[]{:S(2)}, u32[]{:S(2)}) collective-permute-start(s16[392,384]{1,0:T(8,128)(2,1)S(1)} %get-tuple-element.28), channel_id=1, source_target_pairs={{0,1},{4,5},{11,10},{15,14},{16,17},{20,21},{27,26},{31,30}} | collective-permute-start | bytes 903176 | tf_op jit(solution)/shard_map/ppermute | solution.py:381
  63.3 20.4 %collective-permute-start.7 = (s16[392,384]{1,0:T(8,128)(2,1)S(1)}, s16[392,384]{1,0:T(8,128)(2,1)S(1)}, u32[]{:S(2)}, u32[]{:S(2)}) collective-permute-start(s16[392,384]{1,0:T(8,128)(2,1)S(1)} %shard_map.43), channel_id=1, source_target_pairs={{3,2},{2,1},{7,6},{6,5},{8,9},{9,10},{12,13},{13,14},{19,18},{18,1... | collective-permute-start | bytes 903176 | tf_op jit(solution)/shard_map/ppermute | solution.py:381
  73.1 17.3 %collective-permute-start.15 = (s16[392,384]{1,0:T(8,128)(2,1)S(1)}, s16[392,384]{1,0:T(8,128)(2,1)S(1)}, u32[]{:S(2)}, u32[]{:S(2)}) collective-permute-start(s16[392,384]{1,0:T(8,128)(2,1)S(1)} %shard_map.48), channel_id=1, source_target_pairs={{2,1},{6,5},{9,10},{13,14},{1,2},{5,6},{10,9},{14,13},{18,17},{22,... | collective-permute-start | bytes 903176 | tf_op jit(solution)/shard_map/ppermute | solution.py:381
  75.5 16.5 %collective-permute-start.10 = (s16[392,384]{1,0:T(8,128)(2,1)S(1)}, s16[392,384]{1,0:T(8,128)(2,1)S(1)}, u32[]{:S(2)}, u32[]{:S(2)}) collective-permute-start(s16[392,384]{1,0:T(8,128)(2,1)S(1)} %shard_map.45), channel_id=1, source_target_pairs={{1,2},{5,6},{10,9},{14,13},{17,18},{21,22},{26,25},{30,29}} | collective-permute-start | bytes 903176 | tf_op jit(solution)/shard_map/ppermute | solution.py:381
  81.1 12.6 %collective-permute-start.12 = (s16[392,384]{1,0:T(8,128)(2,1)S(1)}, s16[392,384]{1,0:T(8,128)(2,1)S(1)}, u32[]{:S(2)}, u32[]{:S(2)}) collective-permute-start(s16[392,384]{1,0:T(8,128)(2,1)S(1)} %get-tuple-element.29), channel_id=1, source_target_pairs={{0,1},{3,2},{4,5},{7,6},{11,10},{8,9},{15,14},{12,13},{16,17},{19,... | collective-permute-start | bytes 903176 | tf_op jit(solution)/shard_map/ppermute | solution.py:381
  82.4 16.5 %collective-permute-start.17 = (s16[392,384]{1,0:T(8,128)(2,1)S(1)}, s16[392,384]{1,0:T(8,128)(2,1)S(1)}, u32[]{:S(2)}, u32[]{:S(2)}) collective-permute-start(s16[392,384]{1,0:T(8,128)(2,1)S(1)} %get-tuple-element.31), channel_id=1, source_target_pairs={{3,2},{7,6},{8,9},{12,13},{0,1},{4,5},{11,10},{15,14},{19,18},{23,... | collective-permute-start | bytes 903176 | tf_op jit(solution)/shard_map/ppermute | solution.py:381
  83.9 16.5 %collective-permute-start.8 = (s16[392,384]{1,0:T(8,128)(2,1)S(1)}, s16[392,384]{1,0:T(8,128)(2,1)S(1)}, u32[]{:S(2)}, u32[]{:S(2)}) collective-permute-start(s16[392,384]{1,0:T(8,128)(2,1)S(1)} %shard_map.44), channel_id=1, source_target_pairs={{2,1},{1,0},{6,5},{5,4},{9,10},{10,11},{13,14},{14,15},{18,17},{17... | collective-permute-start | bytes 903176 | tf_op jit(solution)/shard_map/ppermute | solution.py:381
  90.6 17.0 %collective-permute-start.16 = (s16[392,384]{1,0:T(8,128)(2,1)S(1)}, s16[392,384]{1,0:T(8,128)(2,1)S(1)}, u32[]{:S(2)}, u32[]{:S(2)}) collective-permute-start(s16[392,384]{1,0:T(8,128)(2,1)S(1)} %shard_map.49), channel_id=1, source_target_pairs={{1,0},{5,4},{10,11},{14,15},{2,3},{6,7},{9,8},{13,12},{17,16},{21,... | collective-permute-start | bytes 903176 | tf_op jit(solution)/shard_map/ppermute | solution.py:381
  92.2 15.2 %copy-start.4 = (f32[384,768]{1,0:T(8,128)S(1)}, f32[384,768]{1,0:T(8,128)}, u32[]{:S(2)}) copy-start(f32[384,768]{1,0:T(8,128)} %front.1) | copy-start | bytes 3538948
  92.2 15.4 %collective-permute-start.11 = (s16[392,384]{1,0:T(8,128)(2,1)S(1)}, s16[392,384]{1,0:T(8,128)(2,1)S(1)}, u32[]{:S(2)}, u32[]{:S(2)}) collective-permute-start(s16[392,384]{1,0:T(8,128)(2,1)S(1)} %shard_map.46), channel_id=1, source_target_pairs={{2,3},{6,7},{9,8},{13,12},{18,19},{22,23},{25,24},{29,28}} | collective-permute-start | bytes 903176 | tf_op jit(solution)/shard_map/ppermute | solution.py:381
  93.7 14.0 %collective-permute-start.19 = (s16[392,384]{1,0:T(8,128)(2,1)S(1)}, s16[392,384]{1,0:T(8,128)(2,1)S(1)}, u32[]{:S(2)}, u32[]{:S(2)}) collective-permute-start(s16[392,384]{1,0:T(8,128)(2,1)S(1)} %get-tuple-element.32), channel_id=1, source_target_pairs={{0,1},{4,5},{11,10},{15,14},{3,2},{7,6},{8,9},{12,13},{16,17},{20,... | collective-permute-start | bytes 903176 | tf_op jit(solution)/shard_map/ppermute | solution.py:381
  98.9 14.3 %collective-permute-start.13 = (s16[392,384]{1,0:T(8,128)(2,1)S(1)}, s16[392,384]{1,0:T(8,128)(2,1)S(1)}, u32[]{:S(2)}, u32[]{:S(2)}) collective-permute-start(s16[392,384]{1,0:T(8,128)(2,1)S(1)} %shard_map.47), channel_id=1, source_target_pairs={{1,2},{5,6},{10,9},{14,13},{17,18},{21,22},{26,25},{30,29}} | collective-permute-start | bytes 903176 | tf_op jit(solution)/shard_map/ppermute | solution.py:381
  100.4 17.1 %collective-permute-start.18 = (s16[392,384]{1,0:T(8,128)(2,1)S(1)}, s16[392,384]{1,0:T(8,128)(2,1)S(1)}, u32[]{:S(2)}, u32[]{:S(2)}) collective-permute-start(s16[392,384]{1,0:T(8,128)(2,1)S(1)} %shard_map.50), channel_id=1, source_target_pairs={{2,1},{6,5},{9,10},{13,14},{1,2},{5,6},{10,9},{14,13},{18,17},{22,... | collective-permute-start | bytes 903176 | tf_op jit(solution)/shard_map/ppermute | solution.py:381
  (1 other events, 1.2 us)

commit v3 on v1

v3 whole, which is shorter than its diff:
```python
import functools

import jax
import jax.numpy as jnp
from jax import lax
from jax.experimental import pallas as pl
from jax.experimental.pallas import tpu as pltpu
from jax.sharding import PartitionSpec as P


WIDTH = 1024
GROUP = 64
CODES = 8
STEPS = 256.0
TOP = 32767.0


def plain(panels, sizes, front):
    piece_rows = panels.shape[0]
    panel_count = panels.shape[1] // WIDTH
    first = lax.axis_index("gz") * panel_count
    limits = lax.dynamic_slice_in_dim(sizes, first, panel_count, 0)
    column = jnp.arange(WIDTH, dtype=jnp.int32)
    live = (column[None, :] < limits[:, None]).reshape(panel_count * WIDTH).astype(jnp.bfloat16)
    gathered = lax.all_gather(panels, ("gx", "gy"), axis=0, tiled=True)
    count_x = lax.axis_size("gx")
    count_y = lax.axis_size("gy")
    block_rows = piece_rows * count_y
    row_part = lax.dynamic_slice_in_dim(gathered, lax.axis_index("gx") * block_rows, block_rows, 0)
    grouped = gathered.reshape(count_x, count_y, piece_rows, panels.shape[1])
    column_part = lax.dynamic_index_in_dim(grouped, lax.axis_index("gy"), 1, keepdims=False)
    column_part = column_part.reshape(count_x * piece_rows, panels.shape[1])
    masked = row_part * live[None, :]
    summed = lax.psum_scatter(
        -lax.dot_general(
            masked, column_part, (((1,), (1,)), ((), ())), preferred_element_type=jnp.float32
        ),
        "gz",
        scatter_dimension=0,
        tiled=True,
    )
    return front + summed


def place(rnd, n):
    g = lax.axis_index("gy")
    z = lax.axis_index("gz")
    own_half = g // (n // 2)
    half = own_half if rnd == 0 else 1 - own_half
    w = jnp.where(half == 1, z, n - 1 - z)
    far = jnp.where(half == 1, n - 1, 0)
    return g, w, far


def product(rows, cols):
    return lax.dot_general(rows, cols[...], (((1,), (1,)), ((), ())), preferred_element_type=jnp.float32)


def decode(packet_ref, group, codes):
    scale = jnp.exp2(codes[group : group + 1, :] * (1.0 / STEPS)) * (1.0 / TOP)
    values = packet_ref[group * GROUP : (group + 1) * GROUP, :].astype(jnp.int32).astype(jnp.float32)
    return values * scale


def read_codes(packet_ref):
    height = packet_ref.shape[0] - CODES
    return packet_ref[height:, :].astype(jnp.int32).astype(jnp.float32)


def encode(out_ref, read):
    height, width = out_ref.shape[0] - CODES, out_ref.shape[1]
    line = lax.broadcasted_iota(jnp.int32, (CODES, width), 0)
    codes = jnp.zeros((CODES, width), jnp.float32)
    for group in range(height // GROUP):
        part = read(group)
        most = jnp.max(jnp.abs(part), axis=0, keepdims=True)
        code = jnp.ceil(jnp.log2(jnp.maximum(most, 1e-30)) * STEPS) + 1.0
        scaled = jnp.round(part * (jnp.exp2(code * (-1.0 / STEPS)) * TOP))
        scaled = jnp.clip(scaled, -TOP, TOP)
        out_ref[group * GROUP : (group + 1) * GROUP, :] = scaled.astype(jnp.int32).astype(jnp.int16)
        codes = jnp.where(line == group, code, codes)
    out_ref[height:, :] = codes.astype(jnp.int32).astype(jnp.int16)


def rows_of(group):
    return slice(group * GROUP, (group + 1) * GROUP)


def rows_of(group):
    return slice(group * GROUP, (group + 1) * GROUP)


def headed(to, n):
    g = lax.axis_index("gy")
    return jnp.where(g // (n // 2) == to // (n // 2), 0, 1)


def at_ends(n):
    g = lax.axis_index("gy")
    return (g == 0) | (g == n - 1)


def own_kernel(n, live, panels, beside, cols, sums, locals_, packet, other):
    _, w, _ = place(0, n)
    ends = at_ends(n)
    for index, pick in ((0, ends), (1, jnp.logical_not(ends))):
        locals_[index] = jnp.where(pick, panels[...], beside[...]) * live[...]
        sums[index] = product(locals_[index], cols)
    at = jnp.where((w == 0) | (w == 2), 0, 1)
    encode(packet, lambda group: sums[at, rows_of(group), :])

    @pl.when(w < 2)
    def _():
        encode(other, lambda group: sums[1 - at, rows_of(group), :])


def far_kernel(n, live, first, second, cols, sums, kept, packet):
    kept[...] = jnp.where(at_ends(n), second[...], first[...]) * live[...]
    sums[...] = product(kept[...], cols)
    encode(packet, lambda group: sums[rows_of(group), :])


def near_kernel(kept, cols, sums, packet):
    sums[...] = product(kept[...], cols)
    encode(packet, lambda group: sums[rows_of(group), :])


def near_step_kernel(n, sums, held, packet):
    _, w, _ = place(1, n)

    @pl.when(w == 1)
    def _():
        codes = read_codes(held)
        encode(packet, lambda group: sums[rows_of(group), :] + decode(held, group, codes))


def early(kind, n):
    z = lax.axis_index("gz")
    top = n - 1 if kind == "xf" else n - 2
    return jnp.where(z < n // 2, headed(top, n), headed(n - 1 - top, n))


def at_edge(n):
    z = lax.axis_index("gz")
    return (z == 0) | (z == n - 1)


def crossed_kernel(kind, is_early, makes, n, *rest):
    if makes:
        live, locals_, first, second, cols, sums, packet, kept = rest
        kept[...] = jnp.where(at_ends(n), first[...], second[...]) * live[...]
    else:
        locals_, kept, cols, sums, *packet = rest
        packet = packet[0] if packet else None
    at = early(kind, n) if is_early else 1 - early(kind, n)

    @pl.when(at == 0)
    def _():
        sums[...] = product(locals_[0 if kind == "xf" else 1], cols)

    @pl.when(at == 1)
    def _():
        sums[...] = product(kept[...], cols)

    if packet is not None:

        @pl.when(at_edge(n))
        def _():
            encode(packet, lambda group: sums[rows_of(group), :])


def crossed_step_kernel(n, sums, held, packet):
    @pl.when(jnp.logical_not(at_edge(n)))
    def _():
        codes = read_codes(held)
        encode(packet, lambda group: sums[rows_of(group), :] + decode(held, group, codes))


def last_kernel(n, far_late, held, near_late, packet):
    @pl.when(at_edge(n))
    def _():
        encode(packet, lambda group: near_late[rows_of(group), :])

    @pl.when(jnp.logical_not(at_edge(n)))
    def _():
        codes = read_codes(held)
        encode(packet, lambda group: far_late[rows_of(group), :] + decode(held, group, codes))


VMEM = pl.BlockSpec(memory_space=pltpu.VMEM)


def call(kernel, outs, operands, flops):
    size = sum(v.size * v.dtype.itemsize for v in (*operands, *outs))
    return pl.pallas_call(
        kernel,
        out_shape=outs if len(outs) > 1 else outs[0],
        in_specs=[VMEM] * len(operands),
        out_specs=[VMEM] * len(outs) if len(outs) > 1 else VMEM,
        compiler_params=pltpu.CompilerParams(vmem_limit_bytes=min(size + (4 << 20), 60 << 20)),
        cost_estimate=pl.CostEstimate(flops=flops, bytes_accessed=size, transcendentals=0),
    )(*operands)


def subtract(out_ref, value_ref, columns, refs):
    codes = [read_codes(ref) for ref in refs]
    for group in range(out_ref.shape[0] // GROUP):
        value = value_ref[rows_of(group), columns]
        for ref, code in zip(refs, codes):
            value = value - decode(ref, group, code)
        out_ref[rows_of(group), columns] = value


def own_columns(count_x, rows, d):
    return pl.ds(pl.multiple_of(lax.rem(lax.axis_index("gx") + d, count_x) * rows, 128), rows)


def base_kernel(n, count_x, front, *rest):
    packets, sums, out_ref = rest[:6], rest[6:-1], rest[-1]
    z = lax.axis_index("gz")
    rows = front.shape[0]
    _, w, _ = place(0, n)
    columns = functools.partial(own_columns, count_x, rows)

    @pl.when(w >= n // 2)
    def _():
        at = jnp.where(w == n - 1, 0, 1)
        out_ref[:, columns(0)] = front[:, columns(0)] - sums[0][at]
        subtract(out_ref, out_ref, columns(0), packets[:3])

    @pl.when(w == 0)
    def _():
        out_ref[:, columns(0)] = front[:, columns(0)] - sums[1][...]
        subtract(out_ref, out_ref, columns(0), packets[3:])

    @pl.when(w == 1)
    def _():
        out_ref[:, columns(0)] = front[:, columns(0)] - sums[2][...]

    edge = (z == 0) | (z == n - 1)
    for d in range(1, count_x):
        for side, index in ((edge, 1 + 2 * d), (jnp.logical_not(edge), 2 + 2 * d)):

            @pl.when(side)
            def _(d=d, index=index):
                out_ref[:, columns(d)] = front[:, columns(d)] - sums[index][...]


def final_kernel(n, count_x, base, *rest):
    packets, out_ref = rest[:-1], rest[-1]
    z = lax.axis_index("gz")
    rows = base.shape[0]
    _, w, _ = place(0, n)
    columns = functools.partial(own_columns, count_x, rows)

    @pl.when(w == 1)
    def _():
        subtract(out_ref, base, columns(0), packets[:2])

    @pl.when(w != 1)
    def _():
        out_ref[:, columns(0)] = base[:, columns(0)]

    edge = (z == 0) | (z == n - 1)
    for d in range(1, count_x):
        for side, refs in ((edge, packets[2 * d : 2 * d + 1]), (jnp.logical_not(edge), packets[2 * d : 2 * d + 2])):

            @pl.when(side)
            def _(d=d, refs=refs):
                subtract(out_ref, base, columns(d), refs)


def plan(count_x):
    crossed = range(1, count_x)
    names = [">beside", ">far0"] + [f">cross{d}" for d in crossed] + [">near0"]
    names += ["own_k", ">own_a", ">own_b", ">own_c", ">far1", "far_k", ">far_a", ">far_b", ">far_c", ">near1"]
    for d in crossed:
        names += [f"xf{d}_k", f">xf{d}_0"]
    for d in crossed:
        names += [f"xn{d}_k", f">xn{d}_0"]
    names += ["near_k", ">near_0"]
    for d in crossed:
        names += [f"xf{d}_j1", f">xf{d}_1", f"xn{d}_m", f"xf{d}_m"]
    for d in crossed:
        names += [f"xn{d}_j1", f">xn{d}_1"]
    for d in crossed:
        names += [f"last{d}_k", f">last{d}_0"]
    return names + ["base", "near_j1", ">near_1", "final"]


def shards(n, count_x, panels, sizes, front):
    rows, width = panels.shape
    square = 2 * rows * rows * width
    one_sum = jax.ShapeDtypeStruct((rows, rows), jnp.float32)
    piece_like = jax.ShapeDtypeStruct((rows, width), jnp.bfloat16)

    block = jax.ShapeDtypeStruct(front.shape, jnp.float32)

    def way(rnd, hops):
        pairs = []
        for g in range(n):
            half = g // (n // 2) if rnd == 0 else 1 - g // (n // 2)
            for a, b in hops:
                source, target = (a, b) if half == 1 else (n - 1 - a, n - 1 - b)
                pairs.append((g * n + source, g * n + target))
        return pairs

    def both(hop):
        return way(0, [hop]) + way(1, [hop])

    count = width // WIDTH
    here = jnp.arange(sizes.size, dtype=jnp.int32)[:, None] == lax.axis_index("gz") * count + jnp.arange(count)[None, :]
    limits = jnp.sum(jnp.where(here, sizes[:, None], 0), axis=0)
    live = (jnp.arange(WIDTH)[None, :] < limits[:, None]).reshape(1, width).astype(jnp.bfloat16)

    hops = {
        "own_a": way(0, [(0, 3), (1, 2)]),
        "own_b": way(0, [(0, 2), (1, 3)]),
        "own_c": way(0, [(2, 3), (3, 2)]),
        "far_a": way(1, [(0, 3)]),
        "far_b": way(1, [(1, 3)]),
        "far_c": way(1, [(2, 3)]),
        "near_0": way(1, [(0, 1), (3, 2)]),
        "near_1": way(1, [(1, 2)]),
        "xf_0": both((0, 1)),
        "xf_1": both((1, 2)),
        "last_0": both((2, 3)) + both((3, 2)),
        "xn_0": both((0, 1)),
        "xn_1": both((1, 2)),
    }
    y_moves = {
        "beside": (None, [(g, g ^ 1) for g in range(n)]),
        "far0": (None, [(0, 2), (3, 1)]),
        "near0": ("beside", [(0, 3), (3, 0)]),
        "far1": ("far0", [(2, 3), (1, 0)]),
        "near1": ("near0", [(3, 2), (0, 1)]),
    }
    held = {}
    sums = {}
    sent = {}
    got = {}
    pair_of_sums = jax.ShapeDtypeStruct((2, rows, rows), jnp.float32)
    packet = jax.ShapeDtypeStruct((rows + CODES, rows), jnp.int16)
    for name in plan(count_x):
        label = name.lstrip(">")
        part, _, step = label.partition("_")
        kind, d = part.rstrip("0123456789"), int("0" + part.lstrip("abcdefghijklmnopqrstuvwxyz"))
        if label in y_moves:
            source, pairs = y_moves[label]
            held[label] = lax.ppermute(panels if source is None else held[source], "gy", pairs)
        elif kind == "cross":
            held[label] = lax.ppermute(panels, "gx", [((i + d) % count_x, i) for i in range(count_x)])
        elif name[0] == ">":
            got[label] = lax.ppermute(sent[label], ("gy", "gz"), hops[f"{kind}_{step}"])
        elif label == "base":
            each = [got[f"{k}_{i}"] for k in ("own", "far") for i in "abc"]
            each += [sums[k] for k in ("own", "far", "near")]
            each += [sums[f"{k}{d}", "late"] for d in range(1, count_x) for k in ("xf", "xn")]
            base = call(functools.partial(base_kernel, n, count_x), [block], [front, *each], 1)
        elif label == "final":
            each = [got["near_0"], got["near_1"]]
            for d in range(1, count_x):
                each += [got[f"last{d}_0"], got[f"xn{d}_1"]]
            return call(functools.partial(final_kernel, n, count_x), [block], [base, *each], 1)
        elif step[0] == "j":
            at = int(step[1])
            kernel = near_step_kernel if kind == "near" else crossed_step_kernel
            which = part if kind == "near" else (part, "early" if at == 1 else "late")
            before = got[f"{part}_{at - 1}"]
            sent[f"{part}_{at}"] = call(functools.partial(kernel, n), [packet], [sums[which], before], 1)
        elif kind == "last":
            sent[f"{part}_0"] = call(
                functools.partial(last_kernel, n),
                [packet],
                [sums[f"xf{d}", "late"], got[f"xf{d}_1"], sums[f"xn{d}", "late"]],
                1,
            )
        elif kind == "own":
            sums[part], held["locals"], sent["own_a"], sent["own_b"] = call(
                functools.partial(own_kernel, n),
                [pair_of_sums, jax.ShapeDtypeStruct((2, rows, width), jnp.bfloat16), packet, packet],
                [live, panels, held["beside"], panels],
                2 * square,
            )
            sent["own_c"] = sent["own_a"]
        elif kind == "far":
            sums[part], held["kept_far"], sent["far_a"] = call(
                functools.partial(far_kernel, n),
                [one_sum, piece_like, packet],
                [live, held["far0"], held["far1"], panels],
                square,
            )
            sent["far_b"] = sent["far_c"] = sent["far_a"]
        elif kind == "near":
            sums[part], sent["near_0"] = call(near_kernel, [one_sum, packet], [held["kept_near"], panels], square)
        else:
            is_early = step == "k"
            kept = "kept_far" if kind == "xf" else "kept_near"
            makes = kept not in held
            pieces = [held["near0"], held["near1"]] if makes else [held[kept]]
            packs = is_early
            done = call(
                functools.partial(crossed_kernel, kind, is_early, makes, n),
                [one_sum] + [packet] * packs + [piece_like] * makes,
                [live] * makes + [held["locals"], *pieces, held[f"cross{d}"]],
                square,
            )
            done = done if isinstance(done, (tuple, list)) else [done]
            sums[part, "early" if is_early else "late"] = done[0]
            if packs:
                sent[f"{part}_0"] = done[1]
            if makes:
                held[kept] = done[2]


def solution(mesh):
    n, count_x = mesh.shape["gz"], mesh.shape["gx"]
    in_specs = (P(("gx", "gy"), "gz"), P(), P(("gx", "gz"), "gy"))
    out_specs = P(("gx", "gz"), "gy")
    if n != 4 or mesh.shape["gy"] != n or count_x < 2:
        return jax.shard_map(plain, mesh=mesh, in_specs=in_specs, out_specs=out_specs, check_vma=False)

    def body(panels, sizes, front):
        return shards(n, count_x, panels, sizes, front)

    return jax.shard_map(body, mesh=mesh, in_specs=in_specs, out_specs=out_specs, check_vma=False)
```

time: 104 us -> 127 us (1.22)
  the two profiles are of different devices: /device:TPU:15 before, /device:TPU:16 now
where the time goes in v3:
time: 127 us; the launch traced here: 126 us
  waiting for transfers between devices  71 us (56%)
  starting transfers between devices  35.9 us (28%)
  Pallas kernels  14 us (11%)
  local copies, waits for them, and re-layouts  4.03 us (3%)
    ppermute x13, waiting for transfers between devices, shards(): got[label] = lax.ppermute(sent[label], ('gy', 'gz'), hops[f'{kind}_{step}'])  34 us
    ppermute x5, waiting for transfers between devices, shards(): lax.ppermute(panels if source is None else held[source], 'gy', pairs)  28 us
    ppermute x13, starting transfers between devices, shards(): got[label] = lax.ppermute(sent[label], ('gy', 'gz'), hops[f'{kind}_{step}'])  23.8 us
    pallas_call x13, Pallas kernels, call(): pl.pallas_call(kernel, out_shape=outs if len(outs) > 1 else outs[0], in_s...  14 us
    ppermute x5, starting transfers between devices, shards(): lax.ppermute(panels if source is None else held[source], 'gy', pairs)  10.6 us
    ppermute x1, waiting for transfers between devices, shards(): lax.ppermute(panels, 'gx', [((i + d) % count_x, i) for i in range(count_x)])  9 us
    unnamed x11, local copies, waits for them, and re-layouts  4.03 us
  transfers between devices with their start and end apart: 19, of which 11 were waited for; matrix products, arithmetic and copies ran while one was open for 1% of the time, Pallas kernels for 10%

profile of v3, /device:TPU:16, one launch (start us, length us, event | category | flops | bytes accessed | tf_op | source)
XLA Modules:
  0.0 126.1 jit_solution(17207906478614845348)
XLA Ops:
  0.0 4.6 %collective-permute-start.4 = (bf16[384,2048]{1,0:T(8,128)(2,1)}, bf16[384,2048]{1,0:T(8,128)(2,1)}, u32[]{:S(2)}, u32[]{:S(2)}) collective-permute-start(bf16[384,2048]{1,0:T(8,128)(2,1)} %cols.5), channel_id=1, source_target_pairs={{0,8},{12,4},{1,9},{13,5},{2,10},{14,6},{3,11},{15,7},{16,24},{28,... | collective-permute-start | bytes 4718600 | tf_op jit(solution)/shard_map/ppermute | solution.py:350
  4.6 2.2 %collective-permute-start.9 = (bf16[384,2048]{1,0:T(8,128)(2,1)S(1)}, bf16[384,2048]{1,0:T(8,128)(2,1)S(1)}, u32[]{:S(2)}, u32[]{:S(2)}) collective-permute-start(bf16[384,2048]{1,0:T(8,128)(2,1)S(1)} %collective-permute-done.beside), channel_id=1, source_target_pairs={{0,12},{12,0},{1,13},{13,1},{2,14},{14,2},{3,15},{15,3},{16,28},{2... | collective-permute-start | bytes 4718600 | tf_op jit(solution)/shard_map/ppermute | solution.py:350
  8.1 13.6 %collective-permute-done.4.first = bf16[384,2048]{1,0:T(8,128)(2,1)} collective-permute-done((bf16[384,2048]{1,0:T(8,128)(2,1)}, bf16[384,2048]{1,0:T(8,128)(2,1)}, u32[]{:S(2)}, u32[]{:S(2)}) %collective-permute-start.4) | collective-permute-done | bytes 1572896 | tf_op jit(solution)/shard_map/ppermute | solution.py:350
  22.9 1.6 %collective-permute-start.11 = (bf16[384,2048]{1,0:T(8,128)(2,1)}, bf16[384,2048]{1,0:T(8,128)(2,1)S(1)}, u32[]{:S(2)}, u32[]{:S(2)}) collective-permute-start(bf16[384,2048]{1,0:T(8,128)(2,1)} %cols.5), channel_id=1, source_target_pairs={{16,0},{0,16},{17,1},{1,17},{18,2},{2,18},{19,3},{3,19},{20,4},{4,... | collective-permute-start | bytes 4718600 | tf_op jit(solution)/shard_map/ppermute | solution.py:352
  24.5 14.4 %collective-permute-done.9.rest_2_ = bf16[384,2048]{1,0:T(8,128)(2,1)S(1)} collective-permute-done((bf16[384,2048]{1,0:T(8,128)(2,1)S(1)}, bf16[384,2048]{1,0:T(8,128)(2,1)S(1)}, u32[]{:S(2)}, u32[]{:S(2)}) %collective-permute-start.9) | collective-permute-done | bytes 1572896 | tf_op jit(solution)/shard_map/ppermute | solution.py:350
  38.9 2.5 %collective-permute-start.10 = (bf16[384,2048]{1,0:T(8,128)(2,1)S(1)}, bf16[384,2048]{1,0:T(8,128)(2,1)}, u32[]{:S(2)}, u32[]{:S(2)}) collective-permute-start(bf16[384,2048]{1,0:T(8,128)(2,1)S(1)} %collective-permute-done.9.rest_2_), channel_id=1, source_target_pairs={{12,8},{0,4},{13,9},{1,5},{14,10},{2,6},{15,11},{3,7},{28,24},{16,... | collective-permute-start | bytes 4718600 | tf_op jit(solution)/shard_map/ppermute | solution.py:350
  42.3 1.4 %copy-done = bf16[384,2048]{1,0:T(8,128)(2,1)S(1)} copy-done((bf16[384,2048]{1,0:T(8,128)(2,1)S(1)}, bf16[384,2048]{1,0:T(8,128)(2,1)}, u32[]{:S(2)}) %copy-start) | copy-done | bytes 1572888
  43.7 1.4 %copy-done.3 = bf16[384,2048]{1,0:T(8,128)(2,1)S(1)} copy-done((bf16[384,2048]{1,0:T(8,128)(2,1)S(1)}, bf16[384,2048]{1,0:T(8,128)(2,1)}, u32[]{:S(2)}) %copy-start.3) | copy-done | bytes 1572888
  45.1 2.1 %shard_map.37 = (f32[2,384,384]{2,1,0:T(8,128)S(1)}, bf16[2,384,2048]{2,1,0:T(8,128)(2,1)S(1)}, s16[392,384]{1,0:T(8,128)(2,1)S(1)}, s16[392,384]{1,0:T(8,128)(2,1)S(1)}) custom-call(bf16[1,2048]{1,0:T(2,128)(2,1)S(1)} %bitcast.4, bf16[384,2048]{1,0:T(8,128)(2,1)S(1)} %copy-done, bf16[384,2048]{1,0:T(8,128)(2,1)S(1)} %copy-done.3, bf16[384,2048]{1,0:T(8,128)(2,1)S(1)} %copy-done), custom_call_target="tpu_custom_call" | custom-call | flops 1207959552 | bytes 9650176 | tf_op jit(solution)/shard_map/pallas_call | solution.py:195
  47.3 3.0 %shard_map.38 = (f32[384,384]{1,0:T(8,128)S(1)}, bf16[384,2048]{1,0:T(8,128)(2,1)S(1)}, s16[392,384]{1,0:T(8,128)(2,1)S(1)}) custom-call(bf16[1,2048]{1,0:T(2,128)(2,1)S(1)} %bitcast.5, bf16[384,2048]{1,0:T(8,128)(2,1)} %collective-permute-done.4.first, bf16[384,2048]{1,0:T(8,128)(2,1)} %collective-permute-done.5.second, bf16[384,2048]{1,0:T(8,128)(2,1)S(1)} %copy-done.1), custom_call_target="tpu_custom_call" | custom-call | flops 603979776 | bytes 7186432 | tf_op jit(solution)/shard_map/pallas_call | solution.py:195
  50.3 9.0 %collective-permute-done.11.rest_4_.rest_2_ = bf16[384,2048]{1,0:T(8,128)(2,1)S(1)} collective-permute-done((bf16[384,2048]{1,0:T(8,128)(2,1)}, bf16[384,2048]{1,0:T(8,128)(2,1)S(1)}, u32[]{:S(2)}, u32[]{:S(2)}) %collective-permute-start.11) | collective-permute-done | bytes 1572896 | tf_op jit(solution)/shard_map/ppermute | solution.py:352
  61.6 10.5 %collective-permute-done.14.held = s16[392,384]{1,0:T(8,128)(2,1)S(1)} collective-permute-done((s16[392,384]{1,0:T(8,128)(2,1)S(1)}, s16[392,384]{1,0:T(8,128)(2,1)S(1)}, u32[]{:S(2)}, u32[]{:S(2)}) %collective-permute-start.14) | collective-permute-done | bytes 301088 | tf_op jit(solution)/shard_map/ppermute | solution.py:354
  72.3 2.4 %collective-permute-start.15 = (s16[392,384]{1,0:T(8,128)(2,1)S(1)}, s16[392,384]{1,0:T(8,128)(2,1)S(1)}, u32[]{:S(2)}, u32[]{:S(2)}) collective-permute-start(s16[392,384]{1,0:T(8,128)(2,1)S(1)} %shard_map.46), channel_id=1, source_target_pairs={{2,1},{6,5},{9,10},{13,14},{1,2},{5,6},{10,9},{14,13},{18,17},{22,... | collective-permute-start | bytes 903176 | tf_op jit(solution)/shard_map/ppermute | solution.py:354
  74.7 2.6 %shard_map.39 = (f32[384,384]{1,0:T(8,128)S(1)}, s16[392,384]{1,0:T(8,128)(2,1)S(1)}, bf16[384,2048]{1,0:T(8,128)(2,1)S(1)}) custom-call(bf16[1,2048]{1,0:T(2,128)(2,1)S(1)} %bitcast.6, bf16[2,384,2048]{2,1,0:T(8,128)(2,1)S(1)} %get-tuple-element.24.rest_1_.rest_0_, bf16[384,2048]{1,0:T(8,128)(2,1)S(1)} %collective-permute-done.9.rest_2_, ...), custom_call_target="tpu_custom_call" | custom-call | flops 603979776 | bytes 10332160 | tf_op jit(solution)/shard_map/pallas_call | solution.py:195
  79.6 3.5 %collective-permute-start.1 = (s16[392,384]{1,0:T(8,128)(2,1)S(1)}, s16[392,384]{1,0:T(8,128)(2,1)S(1)}, u32[]{:S(2)}, u32[]{:S(2)}) collective-permute-start(s16[392,384]{1,0:T(8,128)(2,1)S(1)} %get-tuple-element.19), channel_id=1, source_target_pairs={{3,0},{2,1},{7,4},{6,5},{8,11},{9,10},{12,15},{13,14},{19,16},{18,... | collective-permute-start | bytes 903176 | tf_op jit(solution)/shard_map/ppermute | solution.py:354
  85.2 4.6 %collective-permute-start.2 = (s16[392,384]{1,0:T(8,128)(2,1)S(1)}, s16[392,384]{1,0:T(8,128)(2,1)S(1)}, u32[]{:S(2)}, u32[]{:S(2)}) collective-permute-start(s16[392,384]{1,0:T(8,128)(2,1)S(1)} %get-tuple-element.20), channel_id=1, source_target_pairs={{3,1},{2,0},{7,5},{6,4},{8,10},{9,11},{12,14},{13,15},{19,17},{18,... | collective-permute-start | bytes 903176 | tf_op jit(solution)/shard_map/ppermute | solution.py:354
  93.3 3.8 %collective-permute-done.1.rest_0_ = s16[392,384]{1,0:T(8,128)(2,1)S(1)} collective-permute-done((s16[392,384]{1,0:T(8,128)(2,1)S(1)}, s16[392,384]{1,0:T(8,128)(2,1)S(1)}, u32[]{:S(2)}, u32[]{:S(2)}) %collective-permute-start.1) | collective-permute-done | bytes 301088 | tf_op jit(solution)/shard_map/ppermute | solution.py:354
  97.8 5.4 %collective-permute-done.17.held = s16[392,384]{1,0:T(8,128)(2,1)S(1)} collective-permute-done((s16[392,384]{1,0:T(8,128)(2,1)S(1)}, s16[392,384]{1,0:T(8,128)(2,1)S(1)}, u32[]{:S(2)}, u32[]{:S(2)}) %collective-permute-start.17) | collective-permute-done | bytes 301088 | tf_op jit(solution)/shard_map/ppermute | solution.py:354
  103.2 1.5 %collective-permute-start.8 = (s16[392,384]{1,0:T(8,128)(2,1)S(1)}, s16[392,384]{1,0:T(8,128)(2,1)S(1)}, u32[]{:S(2)}, u32[]{:S(2)}) collective-permute-start(s16[392,384]{1,0:T(8,128)(2,1)S(1)} %get-tuple-element.21), channel_id=1, source_target_pairs={{2,3},{6,7},{9,8},{13,12},{18,19},{22,23},{25,24},{29,28}} | collective-permute-start | bytes 903176 | tf_op jit(solution)/shard_map/ppermute | solution.py:354
  105.0 3.9 %collective-permute-done.2.rest_1_ = s16[392,384]{1,0:T(8,128)(2,1)S(1)} collective-permute-done((s16[392,384]{1,0:T(8,128)(2,1)S(1)}, s16[392,384]{1,0:T(8,128)(2,1)S(1)}, u32[]{:S(2)}, u32[]{:S(2)}) %collective-permute-start.2) | collective-permute-done | bytes 301088 | tf_op jit(solution)/shard_map/ppermute | solution.py:354
  110.2 4.6 %collective-permute-start.18 = (s16[392,384]{1,0:T(8,128)(2,1)S(1)}, s16[392,384]{1,0:T(8,128)(2,1)S(1)}, u32[]{:S(2)}, u32[]{:S(2)}) collective-permute-start(s16[392,384]{1,0:T(8,128)(2,1)S(1)} %shard_map.48), channel_id=1, source_target_pairs={{2,1},{6,5},{9,10},{13,14},{1,2},{5,6},{10,9},{14,13},{18,17},{22,... | collective-permute-start | bytes 903176 | tf_op jit(solution)/shard_map/ppermute | solution.py:354
  114.8 2.6 %collective-permute-done.8.rest_5_ = s16[392,384]{1,0:T(8,128)(2,1)S(1)} collective-permute-done((s16[392,384]{1,0:T(8,128)(2,1)S(1)}, s16[392,384]{1,0:T(8,128)(2,1)S(1)}, u32[]{:S(2)}, u32[]{:S(2)}) %collective-permute-start.8) | collective-permute-done | bytes 301088 | tf_op jit(solution)/shard_map/ppermute | solution.py:354
  117.5 6.2 %collective-permute-done.16.rest_2_ = s16[392,384]{1,0:T(8,128)(2,1)S(1)} collective-permute-done((s16[392,384]{1,0:T(8,128)(2,1)S(1)}, s16[392,384]{1,0:T(8,128)(2,1)S(1)}, u32[]{:S(2)}, u32[]{:S(2)}) %collective-permute-start.16) | collective-permute-done | bytes 301088 | tf_op jit(solution)/shard_map/ppermute | solution.py:354
  124.8 1.4 %shard_map.49 = f32[384,768]{1,0:T(8,128)} custom-call(f32[384,768]{1,0:T(8,128)S(1)} %shard_map.43.base, s16[392,384]{1,0:T(8,128)(2,1)S(1)} %collective-permute-done.12.held.rest_0_, s16[392,384]{1,0:T(8,128)(2,1)S(1)} %collective-permute-done.13.rest_1_, s16[392,384]{1,0:T(8,128)(2,1)S(1)} %collective-permute-done.16.rest_2_, ...), custom_call_target="tpu_custom_call" | custom-call | flops 1 | bytes 3563520 | tf_op jit(solution)/shard_map/pallas_call | solution.py:195
  (41 shorter events, 17.1 us)
Async XLA Ops:
  0.0 4.6 %collective-permute-start = (bf16[384,2048]{1,0:T(8,128)(2,1)}, bf16[384,2048]{1,0:T(8,128)(2,1)S(1)}, u32[]{:S(2)}, u32[]{:S(2)}) collective-permute-start(bf16[384,2048]{1,0:T(8,128)(2,1)} %cols.5), channel_id=1, source_target_pairs={{0,4},{4,0},{8,12},{12,8},{1,5},{5,1},{9,13},{13,9},{2,6},{6,2},{1... | collective-permute-start | bytes 4718600 | tf_op jit(solution)/shard_map/ppermute | solution.py:350
  0.0 21.7 %collective-permute-start.4 = (bf16[384,2048]{1,0:T(8,128)(2,1)}, bf16[384,2048]{1,0:T(8,128)(2,1)}, u32[]{:S(2)}, u32[]{:S(2)}) collective-permute-start(bf16[384,2048]{1,0:T(8,128)(2,1)} %cols.5), channel_id=1, source_target_pairs={{0,8},{12,4},{1,9},{13,5},{2,10},{14,6},{3,11},{15,7},{16,24},{28,... | collective-permute-start | bytes 4718600 | tf_op jit(solution)/shard_map/ppermute | solution.py:350
  4.6 34.3 %collective-permute-start.9 = (bf16[384,2048]{1,0:T(8,128)(2,1)S(1)}, bf16[384,2048]{1,0:T(8,128)(2,1)S(1)}, u32[]{:S(2)}, u32[]{:S(2)}) collective-permute-start(bf16[384,2048]{1,0:T(8,128)(2,1)S(1)} %collective-permute-done.beside), channel_id=1, source_target_pairs={{0,12},{12,0},{1,13},{13,1},{2,14},{14,2},{3,15},{15,3},{16,28},{2... | collective-permute-start | bytes 4718600 | tf_op jit(solution)/shard_map/ppermute | solution.py:350
  6.9 1.2 copy-start.2
  21.7 25.6 %collective-permute-start.5 = (bf16[384,2048]{1,0:T(8,128)(2,1)}, bf16[384,2048]{1,0:T(8,128)(2,1)}, u32[]{:S(2)}, u32[]{:S(2)}) collective-permute-start(bf16[384,2048]{1,0:T(8,128)(2,1)} %collective-permute-done.4.first), channel_id=1, source_target_pairs={{8,12},{4,0},{9,13},{5,1},{10,14},{6,2},{11,15},{7,3},{24,28},{20,... | collective-permute-start | bytes 4718600 | tf_op jit(solution)/shard_map/ppermute | solution.py:350
  22.9 36.3 %collective-permute-start.11 = (bf16[384,2048]{1,0:T(8,128)(2,1)}, bf16[384,2048]{1,0:T(8,128)(2,1)S(1)}, u32[]{:S(2)}, u32[]{:S(2)}) collective-permute-start(bf16[384,2048]{1,0:T(8,128)(2,1)} %cols.5), channel_id=1, source_target_pairs={{16,0},{0,16},{17,1},{1,17},{18,2},{2,18},{19,3},{3,19},{20,4},{4,... | collective-permute-start | bytes 4718600 | tf_op jit(solution)/shard_map/ppermute | solution.py:352
  38.9 35.8 %collective-permute-start.10 = (bf16[384,2048]{1,0:T(8,128)(2,1)S(1)}, bf16[384,2048]{1,0:T(8,128)(2,1)}, u32[]{:S(2)}, u32[]{:S(2)}) collective-permute-start(bf16[384,2048]{1,0:T(8,128)(2,1)S(1)} %collective-permute-done.9.rest_2_), channel_id=1, source_target_pairs={{12,8},{0,4},{13,9},{1,5},{14,10},{2,6},{15,11},{3,7},{28,24},{16,... | collective-permute-start | bytes 4718600 | tf_op jit(solution)/shard_map/ppermute | solution.py:350
  42.3 1.4 %copy-start = (bf16[384,2048]{1,0:T(8,128)(2,1)S(1)}, bf16[384,2048]{1,0:T(8,128)(2,1)}, u32[]{:S(2)}) copy-start(bf16[384,2048]{1,0:T(8,128)(2,1)} %cols.5) | copy-start | bytes 4718596
  43.7 1.4 %copy-start.3 = (bf16[384,2048]{1,0:T(8,128)(2,1)S(1)}, bf16[384,2048]{1,0:T(8,128)(2,1)}, u32[]{:S(2)}) copy-start(bf16[384,2048]{1,0:T(8,128)(2,1)} %copy-done.2) | copy-start | bytes 4718596
  45.1 2.1 %copy-start.1 = (bf16[384,2048]{1,0:T(8,128)(2,1)S(1)}, bf16[384,2048]{1,0:T(8,128)(2,1)}, u32[]{:S(2)}) copy-start(bf16[384,2048]{1,0:T(8,128)(2,1)} %cols.5) | copy-start | bytes 4718596
  60.3 11.8 %collective-permute-start.14 = (s16[392,384]{1,0:T(8,128)(2,1)S(1)}, s16[392,384]{1,0:T(8,128)(2,1)S(1)}, u32[]{:S(2)}, u32[]{:S(2)}) collective-permute-start(s16[392,384]{1,0:T(8,128)(2,1)S(1)} %get-tuple-element.30), channel_id=1, source_target_pairs={{3,2},{7,6},{8,9},{12,13},{0,1},{4,5},{11,10},{15,14},{19,18},{23,... | collective-permute-start | bytes 903176 | tf_op jit(solution)/shard_map/ppermute | solution.py:354
  72.3 12.8 %collective-permute-start.15 = (s16[392,384]{1,0:T(8,128)(2,1)S(1)}, s16[392,384]{1,0:T(8,128)(2,1)S(1)}, u32[]{:S(2)}, u32[]{:S(2)}) collective-permute-start(s16[392,384]{1,0:T(8,128)(2,1)S(1)} %shard_map.46), channel_id=1, source_target_pairs={{2,1},{6,5},{9,10},{13,14},{1,2},{5,6},{10,9},{14,13},{18,17},{22,... | collective-permute-start | bytes 903176 | tf_op jit(solution)/shard_map/ppermute | solution.py:354
  78.3 11.9 %collective-permute-start.12 = (s16[392,384]{1,0:T(8,128)(2,1)S(1)}, s16[392,384]{1,0:T(8,128)(2,1)S(1)}, u32[]{:S(2)}, u32[]{:S(2)}) collective-permute-start(s16[392,384]{1,0:T(8,128)(2,1)S(1)} %get-tuple-element.28), channel_id=1, source_target_pairs={{0,1},{3,2},{4,5},{7,6},{11,10},{8,9},{15,14},{12,13},{16,17},{19,... | collective-permute-start | bytes 903176 | tf_op jit(solution)/shard_map/ppermute | solution.py:354
  79.6 17.5 %collective-permute-start.1 = (s16[392,384]{1,0:T(8,128)(2,1)S(1)}, s16[392,384]{1,0:T(8,128)(2,1)S(1)}, u32[]{:S(2)}, u32[]{:S(2)}) collective-permute-start(s16[392,384]{1,0:T(8,128)(2,1)S(1)} %get-tuple-element.19), channel_id=1, source_target_pairs={{3,0},{2,1},{7,4},{6,5},{8,11},{9,10},{12,15},{13,14},{19,16},{18,... | collective-permute-start | bytes 903176 | tf_op jit(solution)/shard_map/ppermute | solution.py:354
  83.2 20.0 %collective-permute-start.17 = (s16[392,384]{1,0:T(8,128)(2,1)S(1)}, s16[392,384]{1,0:T(8,128)(2,1)S(1)}, u32[]{:S(2)}, u32[]{:S(2)}) collective-permute-start(s16[392,384]{1,0:T(8,128)(2,1)S(1)} %get-tuple-element.32), channel_id=1, source_target_pairs={{3,2},{7,6},{8,9},{12,13},{0,1},{4,5},{11,10},{15,14},{19,18},{23,... | collective-permute-start | bytes 903176 | tf_op jit(solution)/shard_map/ppermute | solution.py:354
  84.5 20.4 %collective-permute-start.3 = (s16[392,384]{1,0:T(8,128)(2,1)S(1)}, s16[392,384]{1,0:T(8,128)(2,1)S(1)}, u32[]{:S(2)}, u32[]{:S(2)}) collective-permute-start(s16[392,384]{1,0:T(8,128)(2,1)S(1)} %get-tuple-element.19), channel_id=1, source_target_pairs={{1,0},{0,1},{5,4},{4,5},{10,11},{11,10},{14,15},{15,14},{17,16},{1... | collective-permute-start | bytes 903176 | tf_op jit(solution)/shard_map/ppermute | solution.py:354
  85.2 23.8 %collective-permute-start.2 = (s16[392,384]{1,0:T(8,128)(2,1)S(1)}, s16[392,384]{1,0:T(8,128)(2,1)S(1)}, u32[]{:S(2)}, u32[]{:S(2)}) collective-permute-start(s16[392,384]{1,0:T(8,128)(2,1)S(1)} %get-tuple-element.20), channel_id=1, source_target_pairs={{3,1},{2,0},{7,5},{6,4},{8,10},{9,11},{12,14},{13,15},{19,17},{18,... | collective-permute-start | bytes 903176 | tf_op jit(solution)/shard_map/ppermute | solution.py:354
  90.2 20.0 %collective-permute-start.6 = (s16[392,384]{1,0:T(8,128)(2,1)S(1)}, s16[392,384]{1,0:T(8,128)(2,1)S(1)}, u32[]{:S(2)}, u32[]{:S(2)}) collective-permute-start(s16[392,384]{1,0:T(8,128)(2,1)S(1)} %get-tuple-element.21), channel_id=1, source_target_pairs={{0,3},{4,7},{11,8},{15,12},{16,19},{20,23},{27,24},{31,28}} | collective-permute-start | bytes 903176 | tf_op jit(solution)/shard_map/ppermute | solution.py:354
  93.2 24.1 %copy-start.4 = (f32[384,768]{1,0:T(8,128)S(1)}, f32[384,768]{1,0:T(8,128)}, u32[]{:S(2)}) copy-start(f32[384,768]{1,0:T(8,128)} %front.1) | copy-start | bytes 3538948
  97.1 17.7 %collective-permute-start.7 = (s16[392,384]{1,0:T(8,128)(2,1)S(1)}, s16[392,384]{1,0:T(8,128)(2,1)S(1)}, u32[]{:S(2)}, u32[]{:S(2)}) collective-permute-start(s16[392,384]{1,0:T(8,128)(2,1)S(1)} %get-tuple-element.21), channel_id=1, source_target_pairs={{1,3},{5,7},{10,8},{14,12},{17,19},{21,23},{26,24},{30,28}} | collective-permute-start | bytes 903176 | tf_op jit(solution)/shard_map/ppermute | solution.py:354
  103.2 14.2 %collective-permute-start.8 = (s16[392,384]{1,0:T(8,128)(2,1)S(1)}, s16[392,384]{1,0:T(8,128)(2,1)S(1)}, u32[]{:S(2)}, u32[]{:S(2)}) collective-permute-start(s16[392,384]{1,0:T(8,128)(2,1)S(1)} %get-tuple-element.21), channel_id=1, source_target_pairs={{2,3},{6,7},{9,8},{13,12},{18,19},{22,23},{25,24},{29,28}} | collective-permute-start | bytes 903176 | tf_op jit(solution)/shard_map/ppermute | solution.py:354
  104.9 18.8 %collective-permute-start.16 = (s16[392,384]{1,0:T(8,128)(2,1)S(1)}, s16[392,384]{1,0:T(8,128)(2,1)S(1)}, u32[]{:S(2)}, u32[]{:S(2)}) collective-permute-start(s16[392,384]{1,0:T(8,128)(2,1)S(1)} %shard_map.47), channel_id=1, source_target_pairs={{1,0},{5,4},{10,11},{14,15},{2,3},{6,7},{9,8},{13,12},{0,1},{4,5},... | collective-permute-start | bytes 903176 | tf_op jit(solution)/shard_map/ppermute | solution.py:354
  108.9 14.8 %collective-permute-start.13 = (s16[392,384]{1,0:T(8,128)(2,1)S(1)}, s16[392,384]{1,0:T(8,128)(2,1)S(1)}, u32[]{:S(2)}, u32[]{:S(2)}) collective-permute-start(s16[392,384]{1,0:T(8,128)(2,1)S(1)} %shard_map.44), channel_id=1, source_target_pairs={{1,2},{5,6},{10,9},{14,13},{17,18},{21,22},{26,25},{30,29}} | collective-permute-start | bytes 903176 | tf_op jit(solution)/shard_map/ppermute | solution.py:354
  110.2 14.6 %collective-permute-start.18 = (s16[392,384]{1,0:T(8,128)(2,1)S(1)}, s16[392,384]{1,0:T(8,128)(2,1)S(1)}, u32[]{:S(2)}, u32[]{:S(2)}) collective-permute-start(s16[392,384]{1,0:T(8,128)(2,1)S(1)} %shard_map.48), channel_id=1, source_target_pairs={{2,1},{6,5},{9,10},{13,14},{1,2},{5,6},{10,9},{14,13},{18,17},{22,... | collective-permute-start | bytes 903176 | tf_op jit(solution)/shard_map/ppermute | solution.py:354
